TPU v7x, 256 devices: a whole 4x4x8 slice. The times are simulated.
256 devices in a mesh: section: 8 (over y, core), gx: 8 (over z), gy: 4 (over x).
Axes of the slice: x: 4, y: 4, z: 8, core: 2. Of those that a mesh axis runs over, the one named last changes fastest.
Arguments:
- load_index: int32 [8], P('section'), may hold values from 0 to 63
- load_table: float32 [64, 3], replicated, may hold values from -4 to 4
- toughness: float32 [8, 128, 64, 128], P('section', 'gx', 'gy'), may hold values from 0.3 to 3
- clamp_mask: int32 [128, 64, 128], P('gx', 'gy'), may hold values 0 or 1
- load_mask: int32 [128, 64, 128], P('gx', 'gy'), may hold values 0 or 1
- crack_mask: int32 [128, 64, 128], P('gx', 'gy'), may hold values 0 or 1
Outputs:
- displacement: float32 [8, 3, 128, 64, 128], P('section', None, 'gx', 'gy')
- damage: float32 [8, 128, 64, 128], P('section', 'gx', 'gy')
- section_residuals: float32 [8, 8], P('section')
All inputs are finite; a program needn't handle non-finite values. No bound on the sum of `clamp_mask` or of `load_mask` or of `crack_mask` on one device may be relied on, other than what follows from the above.
Results may differ from a plain program's by a relative error of at most 0.0003.
Values sent between devices are 32-bit elements; how exact they have to be, the bound alone decides.
A program may use at most 64 MiB of HBM per device.

v0:
```python
import jax
import jax.numpy as jnp
from jax import lax
from jax.sharding import PartitionSpec as P

lame_lambda = 1.0
shear_modulus = 1.0
relax_weight = 0.6
stiff_floor = 0.001
eigen_guard = 1e-08
neighbour_offsets = ((1, 0, 0), (-1, 0, 0), (0, 1, 0), (0, -1, 0), (0, 0, 1), (0, 0, -1))


def padded_2(block, sides, width):
    for axis, dim in sides:
        count = lax.axis_size(axis)
        forward = [(i, i + 1) for i in range(count - 1)]
        backward = [(target, source) for source, target in forward]
        low = lax.ppermute(
            lax.slice_in_dim(block, block.shape[dim] - width, None, axis=dim), axis, forward
        )
        high = lax.ppermute(lax.slice_in_dim(block, 0, width, axis=dim), axis, backward)
        block = jnp.concatenate([low, block, high], axis=dim)
    return block


def laid_out(blocks, dim):
    shape = list(blocks.shape[1:])
    shape[dim] *= blocks.shape[0]
    return jnp.moveaxis(blocks, 0, dim).reshape(shape)


def copy_for_each(x, axis):
    length = lax.axis_size(axis)
    return lax.all_to_all(jnp.broadcast_to(x[None], (length, *x.shape)), axis, 0, 0, tiled=True)


def gather_directly(x, axis, dim):
    return laid_out(copy_for_each(x, axis), dim)


def taken_together(x, axis):
    everything = copy_for_each(x, axis)
    return jnp.sum(everything, axis=0)


def unit_offset(axis_index, sign):
    return tuple((sign if other == axis_index else 0 for other in range(3)))


def shifted(padded, offset):
    span_first = padded.shape[-3] - 2
    span_second = padded.shape[-2] - 2
    span_third = padded.shape[-1] - 2
    return padded[
        ...,
        1 + offset[0] : 1 + offset[0] + span_first,
        1 + offset[1] : 1 + offset[1] + span_second,
        1 + offset[2] : 1 + offset[2] + span_third,
    ]


def component(field, index):
    return field[..., index, :, :, :]


def elastic_parts(moved_pad, damage_pad):
    stiff_pad = jnp.square(1.0 - damage_pad) + stiff_floor
    centre = shifted(stiff_pad, (0, 0, 0))
    current = shifted(moved_pad, (0, 0, 0))
    laplace = jnp.zeros_like(current)
    weights = jnp.zeros_like(centre)
    for offset in neighbour_offsets:
        face = 0.5 * (centre + shifted(stiff_pad, offset))
        weights = weights + face
        laplace = laplace + jnp.expand_dims(face, -4) * (shifted(moved_pad, offset) - current)
    divergence = jnp.zeros_like(centre)
    pairs = []
    for axis_index in range(3):
        forward = unit_offset(axis_index, 1)
        backward = unit_offset(axis_index, -1)
        part = component(moved_pad, axis_index)
        divergence = divergence + 0.5 * (shifted(part, forward) - shifted(part, backward))
        pairs.append(shifted(stiff_pad, forward) + shifted(stiff_pad, backward))
    flow = centre * divergence
    diagonal = shear_modulus * jnp.expand_dims(weights, -4) + 0.25 * (
        lame_lambda + shear_modulus
    ) * jnp.stack(pairs, axis=-4)
    return (current, laplace, flow, diagonal)


def flow_gradient(flow_pad):
    parts = [
        0.5
        * (
            shifted(flow_pad, unit_offset(axis_index, 1))
            - shifted(flow_pad, unit_offset(axis_index, -1))
        )
        for axis_index in range(3)
    ]
    return jnp.stack(parts, axis=-4)


def spectral_energy(strain_xx, strain_yy, strain_zz, strain_xy, strain_xz, strain_yz):
    middle_value = (strain_xx + strain_yy + strain_zz) / 3.0
    dev_xx = strain_xx - middle_value
    dev_yy = strain_yy - middle_value
    dev_zz = strain_zz - middle_value
    shear_sum = jnp.square(strain_xy) + jnp.square(strain_xz) + jnp.square(strain_yz)
    spread = jnp.square(dev_xx) + jnp.square(dev_yy) + jnp.square(dev_zz) + 2.0 * shear_sum
    radius = jnp.sqrt(spread / 6.0)
    guarded = spread / 6.0 + eigen_guard
    determinant = (
        dev_xx * (dev_yy * dev_zz - jnp.square(strain_yz))
        - strain_xy * (strain_xy * dev_zz - strain_yz * strain_xz)
        + strain_xz * (strain_xy * strain_yz - dev_yy * strain_xz)
    )
    ratio = jnp.clip(determinant / (2.0 * guarded * jnp.sqrt(guarded)), -1.0, 1.0)
    angle = jnp.arccos(ratio) / 3.0
    largest = middle_value + 2.0 * radius * jnp.cos(angle)
    smallest = middle_value + 2.0 * radius * jnp.cos(angle + 2.0 * jnp.pi / 3.0)
    between = 3.0 * middle_value - largest - smallest
    positive = (
        jnp.square(jax.nn.relu(largest))
        + jnp.square(jax.nn.relu(between))
        + jnp.square(jax.nn.relu(smallest))
    )
    return (
        0.5 * lame_lambda * jnp.square(jax.nn.relu(3.0 * middle_value)) + shear_modulus * positive
    )


def damage_update(moved_pad, damage_pad, toughness_cell, crack_cell):
    grads = [
        [
            0.5
            * (
                shifted(component(moved_pad, first), unit_offset(second, 1))
                - shifted(component(moved_pad, first), unit_offset(second, -1))
            )
            for second in range(3)
        ]
        for first in range(3)
    ]
    energy = spectral_energy(
        grads[0][0],
        grads[1][1],
        grads[2][2],
        0.5 * (grads[0][1] + grads[1][0]),
        0.5 * (grads[0][2] + grads[2][0]),
        0.5 * (grads[1][2] + grads[2][1]),
    )
    beside_all = jnp.zeros_like(energy)
    for offset in neighbour_offsets:
        beside_all = beside_all + shifted(damage_pad, offset)
    updated = (2.0 * energy + toughness_cell * beside_all) / (
        toughness_cell + 2.0 * energy + 6.0 * toughness_cell
    )
    return jnp.where(crack_cell > 0.5, 1.0, updated)


def pad_depth(field):
    return jnp.pad(field, [(0, 0)] * (field.ndim - 1) + [(1, 1)])


def cropped(field, margin):
    return field[..., margin : field.shape[-3] - margin, margin : field.shape[-2] - margin, :]


def on_device(load_index, load_table, toughness, clamp_mask, load_mask, crack_mask):
    sections = lax.axis_size("section")
    clamp = clamp_mask.astype(jnp.float32)
    load = load_mask.astype(jnp.float32)
    crack = crack_mask.astype(jnp.float32)
    fixed = jnp.maximum(clamp, load)
    free = 1.0 - fixed
    cells = float(clamp.size * lax.axis_size("gx") * lax.axis_size("gy"))
    picker = (
        load_index[:, None] == jnp.arange(load_table.shape[0], dtype=jnp.int32)[None, :]
    ).astype(jnp.float32)
    load_vectors = jnp.dot(
        picker, load_table, precision=lax.Precision.HIGHEST, preferred_element_type=jnp.float32
    )
    columns = jnp.arange(sections, dtype=jnp.int32)
    rims = padded_2(jnp.stack([clamp, load, jnp.ones_like(clamp)]), (("gx", 1), ("gy", 2)), 2)
    inside_wide = rims[2]
    rims_near = cropped(rims, 1)
    fixed_near = jnp.maximum(jnp.maximum(rims_near[0], rims_near[1]), 1.0 - rims_near[2])
    load_near = rims_near[1]

    def sweep(state, vectors, field):
        padded = pad_depth(padded_2(state, (("gx", 2), ("gy", 3)), 3))
        current, laplace, flow, diagonal = elastic_parts(padded[:, :3], padded[:, 3])
        flow = flow * inside_wide
        gradient = flow_gradient(pad_depth(flow))
        residual = shear_modulus * cropped(laplace, 1) + (lame_lambda + shear_modulus) * gradient
        relaxed = cropped(current, 1) + relax_weight * residual / cropped(diagonal, 1)
        prescribed = load_near[None, None] * vectors[:, :, None, None, None]
        moved_wide = jnp.where(fixed_near[None, None] > 0.5, prescribed, relaxed)
        new_damage = damage_update(pad_depth(moved_wide), cropped(padded[:, 3], 2), field, crack)
        new_moved = cropped(moved_wide, 1)
        residual_inner = cropped(residual, 1)
        squares = jnp.sum(free[None, None] * jnp.square(residual_inner), axis=(1, 2, 3, 4))
        return (jnp.concatenate([new_moved, new_damage[:, None]], axis=1), squares)

    start_moved = load[None, None] * load_vectors[:, :, None, None, None]
    start_state = jnp.concatenate(
        [start_moved, jnp.broadcast_to(crack, (load_vectors.shape[0], 1) + crack.shape)], axis=1
    )
    start_table = jnp.zeros((load_vectors.shape[0], sections), jnp.float32)
    gathered = gather_directly(toughness, "section", 0)
    home = lax.axis_index("section")

    def advance_home(round_index, carry):
        state, table = carry
        column = (home + round_index) % sections
        field = lax.dynamic_index_in_dim(gathered, column, 0, keepdims=False)
        state, squares = sweep(state, load_vectors, field)
        table = table + (columns == column).astype(jnp.float32)[None, :] * squares[:, None]
        return (state, table)

    final_state, table = lax.fori_loop(0, sections, advance_home, (start_state, start_table))
    table = jnp.sqrt(taken_together(table, ("gx", "gy")) / (3.0 * cells))
    return (final_state[:, :3], final_state[:, 3], table)


def solution(mesh):
    in_specs = (
        P("section"),
        P(),
        P("section", "gx", "gy", None),
        P("gx", "gy", None),
        P("gx", "gy", None),
        P("gx", "gy", None),
    )
    out_specs = (
        P("section", None, "gx", "gy", None),
        P("section", "gx", "gy", None),
        P("section", None),
    )
    return jax.shard_map(
        on_device, mesh=mesh, in_specs=in_specs, out_specs=out_specs, check_vma=False
    )
```

profile of v0, /device:TPU:2, one launch (start us, length us, event | category | flops | bytes accessed | tf_op | source)
XLA Modules:
  0.0 272.7 jit_solution(12507520927510009659)
XLA Ops:
  2.6 3.8 %collective-permute-start.4 = (f32[3,2,16,128]{3,2,1,0:T(8,128)S(1)}, f32[3,2,16,128]{3,2,1,0:T(8,128)S(1)}, u32[]{:S(2)}, u32[]{:S(2)}) collective-permute-start(f32[3,2,16,128]{3,2,1,0:T(8,128)S(1)} %get-tuple-element.433), channel_id=1, source_target_pairs={{0,4},{4,8},{8,12},{12,16},{16,20},{20,24},{24,28},{1,5},{5,9},{9,... | collective-permute-start | bytes 147464 | tf_op jit(solution)/shard_map/ppermute | solution.py:19
  8.8 4.6 %all-to-all-start = ((f32[8,1,16,16,128]{4,3,2,1,0:T(8,128)}), f32[8,1,16,16,128]{4,3,2,1,0:T(8,128)S(1)}, u32[]{:S(2)}, u32[]{:S(2)}) async-start(f32[8,1,16,16,128]{4,3,2,1,0:T(8,128)} %broadcast_in_dim.113), calls=%async_computation | async-start | bytes 2097152 | tf_op jit(solution)/shard_map/all_to_all | solution.py:35
  14.5 3.4 %collective-permute-start.6 = (f32[3,20,2,128]{3,2,1,0:T(2,128)S(1)}, f32[3,20,2,128]{3,2,1,0:T(2,128)S(1)}, u32[]{:S(2)}, u32[]{:S(2)}) collective-permute-start(f32[3,20,2,128]{3,2,1,0:T(2,128)S(1)} %get-tuple-element.431), channel_id=1, source_target_pairs={{0,1},{1,2},{2,3},{4,5},{5,6},{6,7},{8,9},{9,10},{10,11},{12,13},{... | collective-permute-start | bytes 184328 | tf_op jit(solution)/shard_map/ppermute | solution.py:19
  17.9 2.4 collective-permute-start.7
  20.8 3.2 %collective-permute-done.7 = f32[3,20,2,128]{3,2,1,0:T(2,128)S(1)} collective-permute-done((f32[3,20,2,128]{3,2,1,0:T(2,128)S(1)}, f32[3,20,2,128]{3,2,1,0:T(2,128)S(1)}, u32[]{:S(2)}, u32[]{:S(2)}) %collective-permute-start.7) | collective-permute-done | bytes 61472 | tf_op jit(solution)/shard_map/ppermute | solution.py:22
  24.2 5.1 %all-to-all-done = f32[8,1,16,16,128]{4,3,2,1,0:T(8,128)S(1)} async-done(((f32[8,1,16,16,128]{4,3,2,1,0:T(8,128)}), f32[8,1,16,16,128]{4,3,2,1,0:T(8,128)S(1)}, u32[]{:S(2)}, u32[]{:S(2)}) %all-to-all-start) | async-done | bytes 1048608 | tf_op jit(solution)/shard_map/all_to_all | solution.py:35
  29.4 225.6 %while.19 = (s32[]{:T(128)}, f32[1,4,16,16,128]{4,3,2,1,0:T(8,128)S(1)}, f32[1,8]{1,0:T(1,128)S(1)}, f32[18,18,128]{2,1,0:T(8,128)S(1)}, f32[1,18,18,128]{3,2,1,...) while((s32[]{:T(128)}, ...), condition=%wide.region_2.3_spmd.clone, body=%wide.region_0.2_spmd.clone.sunk | while | flops 9979785 | bytes 42991660 | solution.py:222
  29.4 4.6 %collective-permute-start = (f32[1,4,3,16,128]{4,3,2,1,0:T(8,128)S(1)}, f32[1,4,3,16,128]{4,3,2,1,0:T(8,128)S(1)}, u32[]{:S(2)}, u32[]{:S(2)}) collective-permute-start(f32[1,4,3,16,128]{4,3,2,1,0:T(8,128)S(1)} %get-tuple-element.540), channel_id=1, source_target_pairs={{0,4},{4,8},{8,12},{12,16},{16,20},{20,24},{24,28},{1,5},{5,9},{9,... | collective-permute-start | bytes 294920 | tf_op jit(solution)/shard_map/while/body/eval_jaxpr/ppermute | solution.py:19
  36.2 4.3 %collective-permute-done.1 = f32[1,4,3,16,128]{4,3,2,1,0:T(8,128)S(1)} collective-permute-done((f32[1,4,3,16,128]{4,3,2,1,0:T(8,128)S(1)}, f32[1,4,3,16,128]{4,3,2,1,0:T(8,128)S(1)}, u32[]{:S(2)}, u32[]{:S(2)}) %collective-permute-start.1) | collective-permute-done | bytes 98336 | tf_op jit(solution)/shard_map/while/body/eval_jaxpr/ppermute | solution.py:22
  40.5 2.4 collective-permute-start.2
  43.0 3.4 %collective-permute-start.3 = (f32[1,4,22,3,128]{4,3,2,1,0:T(4,128)S(1)}, f32[1,4,22,3,128]{4,3,2,1,0:T(4,128)S(1)}, u32[]{:S(2)}, u32[]{:S(2)}) collective-permute-start(f32[1,4,22,3,128]{4,3,2,1,0:T(4,128)S(1)} %get-tuple-element.543), channel_id=1, source_target_pairs={{0,1},{1,2},{2,3},{4,5},{5,6},{6,7},{8,9},{9,10},{10,11},{12,13},{... | collective-permute-start | bytes 405512 | tf_op jit(solution)/shard_map/while/body/eval_jaxpr/ppermute | solution.py:19
  46.4 1.5 collective-permute-done.2
  47.9 2.5 collective-permute-done.3
  55.1 2.1 fusion.92
  58.6 4.8 %collective-permute-start = (f32[1,4,3,16,128]{4,3,2,1,0:T(8,128)S(1)}, f32[1,4,3,16,128]{4,3,2,1,0:T(8,128)S(1)}, u32[]{:S(2)}, u32[]{:S(2)}) collective-permute-start(f32[1,4,3,16,128]{4,3,2,1,0:T(8,128)S(1)} %get-tuple-element.540), channel_id=1, source_target_pairs={{0,4},{4,8},{8,12},{12,16},{16,20},{20,24},{24,28},{1,5},{5,9},{9,... | collective-permute-start | bytes 294920 | tf_op jit(solution)/shard_map/while/body/eval_jaxpr/ppermute | solution.py:19
  65.7 5.5 %collective-permute-done.1 = f32[1,4,3,16,128]{4,3,2,1,0:T(8,128)S(1)} collective-permute-done((f32[1,4,3,16,128]{4,3,2,1,0:T(8,128)S(1)}, f32[1,4,3,16,128]{4,3,2,1,0:T(8,128)S(1)}, u32[]{:S(2)}, u32[]{:S(2)}) %collective-permute-start.1) | collective-permute-done | bytes 98336 | tf_op jit(solution)/shard_map/while/body/eval_jaxpr/ppermute | solution.py:22
  71.2 1.9 collective-permute-start.2
  73.2 3.9 %collective-permute-start.3 = (f32[1,4,22,3,128]{4,3,2,1,0:T(4,128)S(1)}, f32[1,4,22,3,128]{4,3,2,1,0:T(4,128)S(1)}, u32[]{:S(2)}, u32[]{:S(2)}) collective-permute-start(f32[1,4,22,3,128]{4,3,2,1,0:T(4,128)S(1)} %get-tuple-element.543), channel_id=1, source_target_pairs={{0,1},{1,2},{2,3},{4,5},{5,6},{6,7},{8,9},{9,10},{10,11},{12,13},{... | collective-permute-start | bytes 405512 | tf_op jit(solution)/shard_map/while/body/eval_jaxpr/ppermute | solution.py:19
  77.1 1.5 collective-permute-done.2
  78.6 1.9 collective-permute-done.3
  85.2 2.1 fusion.92
  88.7 5.1 %collective-permute-start = (f32[1,4,3,16,128]{4,3,2,1,0:T(8,128)S(1)}, f32[1,4,3,16,128]{4,3,2,1,0:T(8,128)S(1)}, u32[]{:S(2)}, u32[]{:S(2)}) collective-permute-start(f32[1,4,3,16,128]{4,3,2,1,0:T(8,128)S(1)} %get-tuple-element.540), channel_id=1, source_target_pairs={{0,4},{4,8},{8,12},{12,16},{16,20},{20,24},{24,28},{1,5},{5,9},{9,... | collective-permute-start | bytes 294920 | tf_op jit(solution)/shard_map/while/body/eval_jaxpr/ppermute | solution.py:19
  96.1 4.3 %collective-permute-done.1 = f32[1,4,3,16,128]{4,3,2,1,0:T(8,128)S(1)} collective-permute-done((f32[1,4,3,16,128]{4,3,2,1,0:T(8,128)S(1)}, f32[1,4,3,16,128]{4,3,2,1,0:T(8,128)S(1)}, u32[]{:S(2)}, u32[]{:S(2)}) %collective-permute-start.1) | collective-permute-done | bytes 98336 | tf_op jit(solution)/shard_map/while/body/eval_jaxpr/ppermute | solution.py:22
  100.5 1.9 collective-permute-start.2
  102.4 3.9 %collective-permute-start.3 = (f32[1,4,22,3,128]{4,3,2,1,0:T(4,128)S(1)}, f32[1,4,22,3,128]{4,3,2,1,0:T(4,128)S(1)}, u32[]{:S(2)}, u32[]{:S(2)}) collective-permute-start(f32[1,4,22,3,128]{4,3,2,1,0:T(4,128)S(1)} %get-tuple-element.543), channel_id=1, source_target_pairs={{0,1},{1,2},{2,3},{4,5},{5,6},{6,7},{8,9},{9,10},{10,11},{12,13},{... | collective-permute-start | bytes 405512 | tf_op jit(solution)/shard_map/while/body/eval_jaxpr/ppermute | solution.py:19
  106.4 1.5 collective-permute-done.2
  107.9 1.9 collective-permute-done.3
  114.5 2.1 fusion.92
  118.0 3.9 %collective-permute-start = (f32[1,4,3,16,128]{4,3,2,1,0:T(8,128)S(1)}, f32[1,4,3,16,128]{4,3,2,1,0:T(8,128)S(1)}, u32[]{:S(2)}, u32[]{:S(2)}) collective-permute-start(f32[1,4,3,16,128]{4,3,2,1,0:T(8,128)S(1)} %get-tuple-element.540), channel_id=1, source_target_pairs={{0,4},{4,8},{8,12},{12,16},{16,20},{20,24},{24,28},{1,5},{5,9},{9,... | collective-permute-start | bytes 294920 | tf_op jit(solution)/shard_map/while/body/eval_jaxpr/ppermute | solution.py:19
  124.1 4.3 %collective-permute-done.1 = f32[1,4,3,16,128]{4,3,2,1,0:T(8,128)S(1)} collective-permute-done((f32[1,4,3,16,128]{4,3,2,1,0:T(8,128)S(1)}, f32[1,4,3,16,128]{4,3,2,1,0:T(8,128)S(1)}, u32[]{:S(2)}, u32[]{:S(2)}) %collective-permute-start.1) | collective-permute-done | bytes 98336 | tf_op jit(solution)/shard_map/while/body/eval_jaxpr/ppermute | solution.py:22
  128.5 1.9 collective-permute-start.2
  130.4 3.9 %collective-permute-start.3 = (f32[1,4,22,3,128]{4,3,2,1,0:T(4,128)S(1)}, f32[1,4,22,3,128]{4,3,2,1,0:T(4,128)S(1)}, u32[]{:S(2)}, u32[]{:S(2)}) collective-permute-start(f32[1,4,22,3,128]{4,3,2,1,0:T(4,128)S(1)} %get-tuple-element.543), channel_id=1, source_target_pairs={{0,1},{1,2},{2,3},{4,5},{5,6},{6,7},{8,9},{9,10},{10,11},{12,13},{... | collective-permute-start | bytes 405512 | tf_op jit(solution)/shard_map/while/body/eval_jaxpr/ppermute | solution.py:19
  134.4 1.5 collective-permute-done.2
  135.9 1.9 collective-permute-done.3
  142.5 2.1 fusion.92
  146.0 3.1 %collective-permute-start = (f32[1,4,3,16,128]{4,3,2,1,0:T(8,128)S(1)}, f32[1,4,3,16,128]{4,3,2,1,0:T(8,128)S(1)}, u32[]{:S(2)}, u32[]{:S(2)}) collective-permute-start(f32[1,4,3,16,128]{4,3,2,1,0:T(8,128)S(1)} %get-tuple-element.540), channel_id=1, source_target_pairs={{0,4},{4,8},{8,12},{12,16},{16,20},{20,24},{24,28},{1,5},{5,9},{9,... | collective-permute-start | bytes 294920 | tf_op jit(solution)/shard_map/while/body/eval_jaxpr/ppermute | solution.py:19
  151.4 4.3 %collective-permute-done.1 = f32[1,4,3,16,128]{4,3,2,1,0:T(8,128)S(1)} collective-permute-done((f32[1,4,3,16,128]{4,3,2,1,0:T(8,128)S(1)}, f32[1,4,3,16,128]{4,3,2,1,0:T(8,128)S(1)}, u32[]{:S(2)}, u32[]{:S(2)}) %collective-permute-start.1) | collective-permute-done | bytes 98336 | tf_op jit(solution)/shard_map/while/body/eval_jaxpr/ppermute | solution.py:22
  155.7 1.9 collective-permute-start.2
  157.7 3.9 %collective-permute-start.3 = (f32[1,4,22,3,128]{4,3,2,1,0:T(4,128)S(1)}, f32[1,4,22,3,128]{4,3,2,1,0:T(4,128)S(1)}, u32[]{:S(2)}, u32[]{:S(2)}) collective-permute-start(f32[1,4,22,3,128]{4,3,2,1,0:T(4,128)S(1)} %get-tuple-element.543), channel_id=1, source_target_pairs={{0,1},{1,2},{2,3},{4,5},{5,6},{6,7},{8,9},{9,10},{10,11},{12,13},{... | collective-permute-start | bytes 405512 | tf_op jit(solution)/shard_map/while/body/eval_jaxpr/ppermute | solution.py:19
  163.1 1.9 collective-permute-done.3
  169.7 2.1 fusion.92
  173.2 3.1 %collective-permute-start = (f32[1,4,3,16,128]{4,3,2,1,0:T(8,128)S(1)}, f32[1,4,3,16,128]{4,3,2,1,0:T(8,128)S(1)}, u32[]{:S(2)}, u32[]{:S(2)}) collective-permute-start(f32[1,4,3,16,128]{4,3,2,1,0:T(8,128)S(1)} %get-tuple-element.540), channel_id=1, source_target_pairs={{0,4},{4,8},{8,12},{12,16},{16,20},{20,24},{24,28},{1,5},{5,9},{9,... | collective-permute-start | bytes 294920 | tf_op jit(solution)/shard_map/while/body/eval_jaxpr/ppermute | solution.py:19
  178.6 4.3 %collective-permute-done.1 = f32[1,4,3,16,128]{4,3,2,1,0:T(8,128)S(1)} collective-permute-done((f32[1,4,3,16,128]{4,3,2,1,0:T(8,128)S(1)}, f32[1,4,3,16,128]{4,3,2,1,0:T(8,128)S(1)}, u32[]{:S(2)}, u32[]{:S(2)}) %collective-permute-start.1) | collective-permute-done | bytes 98336 | tf_op jit(solution)/shard_map/while/body/eval_jaxpr/ppermute | solution.py:22
  183.0 1.9 collective-permute-start.2
  184.9 3.9 %collective-permute-start.3 = (f32[1,4,22,3,128]{4,3,2,1,0:T(4,128)S(1)}, f32[1,4,22,3,128]{4,3,2,1,0:T(4,128)S(1)}, u32[]{:S(2)}, u32[]{:S(2)}) collective-permute-start(f32[1,4,22,3,128]{4,3,2,1,0:T(4,128)S(1)} %get-tuple-element.543), channel_id=1, source_target_pairs={{0,1},{1,2},{2,3},{4,5},{5,6},{6,7},{8,9},{9,10},{10,11},{12,13},{... | collective-permute-start | bytes 405512 | tf_op jit(solution)/shard_map/while/body/eval_jaxpr/ppermute | solution.py:19
  188.9 1.5 collective-permute-done.2
  190.4 1.9 collective-permute-done.3
  197.0 2.1 fusion.92
  200.5 3.1 %collective-permute-start = (f32[1,4,3,16,128]{4,3,2,1,0:T(8,128)S(1)}, f32[1,4,3,16,128]{4,3,2,1,0:T(8,128)S(1)}, u32[]{:S(2)}, u32[]{:S(2)}) collective-permute-start(f32[1,4,3,16,128]{4,3,2,1,0:T(8,128)S(1)} %get-tuple-element.540), channel_id=1, source_target_pairs={{0,4},{4,8},{8,12},{12,16},{16,20},{20,24},{24,28},{1,5},{5,9},{9,... | collective-permute-start | bytes 294920 | tf_op jit(solution)/shard_map/while/body/eval_jaxpr/ppermute | solution.py:19
  205.8 4.3 %collective-permute-done.1 = f32[1,4,3,16,128]{4,3,2,1,0:T(8,128)S(1)} collective-permute-done((f32[1,4,3,16,128]{4,3,2,1,0:T(8,128)S(1)}, f32[1,4,3,16,128]{4,3,2,1,0:T(8,128)S(1)}, u32[]{:S(2)}, u32[]{:S(2)}) %collective-permute-start.1) | collective-permute-done | bytes 98336 | tf_op jit(solution)/shard_map/while/body/eval_jaxpr/ppermute | solution.py:22
  210.2 1.9 collective-permute-start.2
  212.1 3.9 %collective-permute-start.3 = (f32[1,4,22,3,128]{4,3,2,1,0:T(4,128)S(1)}, f32[1,4,22,3,128]{4,3,2,1,0:T(4,128)S(1)}, u32[]{:S(2)}, u32[]{:S(2)}) collective-permute-start(f32[1,4,22,3,128]{4,3,2,1,0:T(4,128)S(1)} %get-tuple-element.543), channel_id=1, source_target_pairs={{0,1},{1,2},{2,3},{4,5},{5,6},{6,7},{8,9},{9,10},{10,11},{12,13},{... | collective-permute-start | bytes 405512 | tf_op jit(solution)/shard_map/while/body/eval_jaxpr/ppermute | solution.py:19
  216.1 1.5 collective-permute-done.2
  217.6 1.9 collective-permute-done.3
  224.2 2.1 fusion.92
  227.7 3.1 %collective-permute-start = (f32[1,4,3,16,128]{4,3,2,1,0:T(8,128)S(1)}, f32[1,4,3,16,128]{4,3,2,1,0:T(8,128)S(1)}, u32[]{:S(2)}, u32[]{:S(2)}) collective-permute-start(f32[1,4,3,16,128]{4,3,2,1,0:T(8,128)S(1)} %get-tuple-element.540), channel_id=1, source_target_pairs={{0,4},{4,8},{8,12},{12,16},{16,20},{20,24},{24,28},{1,5},{5,9},{9,... | collective-permute-start | bytes 294920 | tf_op jit(solution)/shard_map/while/body/eval_jaxpr/ppermute | solution.py:19
  233.1 4.3 %collective-permute-done.1 = f32[1,4,3,16,128]{4,3,2,1,0:T(8,128)S(1)} collective-permute-done((f32[1,4,3,16,128]{4,3,2,1,0:T(8,128)S(1)}, f32[1,4,3,16,128]{4,3,2,1,0:T(8,128)S(1)}, u32[]{:S(2)}, u32[]{:S(2)}) %collective-permute-start.1) | collective-permute-done | bytes 98336 | tf_op jit(solution)/shard_map/while/body/eval_jaxpr/ppermute | solution.py:22
  237.4 1.9 collective-permute-start.2
  239.4 3.9 %collective-permute-start.3 = (f32[1,4,22,3,128]{4,3,2,1,0:T(4,128)S(1)}, f32[1,4,22,3,128]{4,3,2,1,0:T(4,128)S(1)}, u32[]{:S(2)}, u32[]{:S(2)}) collective-permute-start(f32[1,4,22,3,128]{4,3,2,1,0:T(4,128)S(1)} %get-tuple-element.543), channel_id=1, source_target_pairs={{0,1},{1,2},{2,3},{4,5},{5,6},{6,7},{8,9},{9,10},{10,11},{12,13},{... | collective-permute-start | bytes 405512 | tf_op jit(solution)/shard_map/while/body/eval_jaxpr/ppermute | solution.py:19
  243.3 1.5 collective-permute-done.2
  244.8 1.9 collective-permute-done.3
  251.5 2.1 fusion.92
  255.5 8.0 %all-to-all-start.1 = ((f32[32,1,8]{2,1,0:T(1,128)}), f32[32,1,8]{2,1,0:T(1,128)S(1)}, u32[]{:S(2)}, u32[]{:S(2)}) async-start(f32[32,1,8]{2,1,0:T(1,128)} %broadcast_in_dim.115), calls=%async_computation.1 | async-start | bytes 32768 | tf_op jit(solution)/shard_map/all_to_all | solution.py:35
  265.0 7.1 %all-to-all-done.1 = f32[32,1,8]{2,1,0:T(1,128)S(1)} async-done(((f32[32,1,8]{2,1,0:T(1,128)}), f32[32,1,8]{2,1,0:T(1,128)S(1)}, u32[]{:S(2)}, u32[]{:S(2)}) %all-to-all-start.1) | async-done | bytes 1056 | tf_op jit(solution)/shard_map/all_to_all | solution.py:35
  (259 shorter events, 75.7 us)
Async XLA Ops:
  0.6 13.5 %copy-start = (f32[64,3]{0,1:T(4,128)S(1)}, f32[64,3]{0,1:T(4,128)}, u32[]{:S(2)}) copy-start(f32[64,3]{0,1:T(4,128)} %param.9) | copy-start | bytes 2308
  0.6 7.1 %copy-start.3 = (f32[1,16,16,128]{3,2,1,0:T(8,128)S(1)}, f32[1,16,16,128]{3,2,1,0:T(8,128)}, u32[]{:S(2)}) copy-start(f32[1,16,16,128]{3,2,1,0:T(8,128)} %param.10) | copy-start | bytes 393220
  2.6 11.8 %collective-permute-start.4 = (f32[3,2,16,128]{3,2,1,0:T(8,128)S(1)}, f32[3,2,16,128]{3,2,1,0:T(8,128)S(1)}, u32[]{:S(2)}, u32[]{:S(2)}) collective-permute-start(f32[3,2,16,128]{3,2,1,0:T(8,128)S(1)} %get-tuple-element.433), channel_id=1, source_target_pairs={{0,4},{4,8},{8,12},{12,16},{16,20},{20,24},{24,28},{1,5},{5,9},{9,... | collective-permute-start | bytes 147464 | tf_op jit(solution)/shard_map/ppermute | solution.py:19
  6.4 8.0 %collective-permute-start.5 = (f32[3,2,16,128]{3,2,1,0:T(8,128)S(1)}, f32[3,2,16,128]{3,2,1,0:T(8,128)S(1)}, u32[]{:S(2)}, u32[]{:S(2)}) collective-permute-start(f32[3,2,16,128]{3,2,1,0:T(8,128)S(1)} %get-tuple-element.434), channel_id=1, source_target_pairs={{4,0},{8,4},{12,8},{16,12},{20,16},{24,20},{28,24},{5,1},{9,5},{13... | collective-permute-start | bytes 147464 | tf_op jit(solution)/shard_map/ppermute | solution.py:22
  8.8 5.5 %copy-start.1 = (s32[16,16,128]{2,1,0:T(8,128)S(1)}, s32[16,16,128]{2,1,0:T(8,128)}, u32[]{:S(2)}) copy-start(s32[16,16,128]{2,1,0:T(8,128)} %param.12) | copy-start | bytes 393220
  8.8 5.5 %copy-start.2 = (s32[16,16,128]{2,1,0:T(8,128)S(1)}, s32[16,16,128]{2,1,0:T(8,128)}, u32[]{:S(2)}) copy-start(s32[16,16,128]{2,1,0:T(8,128)} %param.11) | copy-start | bytes 393220
  8.8 5.6 %copy-start.4 = (s32[16,16,128]{2,1,0:T(8,128)S(1)}, s32[16,16,128]{2,1,0:T(8,128)}, u32[]{:S(2)}) copy-start(s32[16,16,128]{2,1,0:T(8,128)} %param.13) | copy-start | bytes 393220
  8.8 20.5 %all-to-all-start = ((f32[8,1,16,16,128]{4,3,2,1,0:T(8,128)}), f32[8,1,16,16,128]{4,3,2,1,0:T(8,128)S(1)}, u32[]{:S(2)}, u32[]{:S(2)}) async-start(f32[8,1,16,16,128]{4,3,2,1,0:T(8,128)} %broadcast_in_dim.113), calls=%async_computation | async-start | bytes 2097152 | tf_op jit(solution)/shard_map/all_to_all | solution.py:35
  14.5 6.3 %collective-permute-start.6 = (f32[3,20,2,128]{3,2,1,0:T(2,128)S(1)}, f32[3,20,2,128]{3,2,1,0:T(2,128)S(1)}, u32[]{:S(2)}, u32[]{:S(2)}) collective-permute-start(f32[3,20,2,128]{3,2,1,0:T(2,128)S(1)} %get-tuple-element.431), channel_id=1, source_target_pairs={{0,1},{1,2},{2,3},{4,5},{5,6},{6,7},{8,9},{9,10},{10,11},{12,13},{... | collective-permute-start | bytes 184328 | tf_op jit(solution)/shard_map/ppermute | solution.py:19
  17.9 6.1 %collective-permute-start.7 = (f32[3,20,2,128]{3,2,1,0:T(2,128)S(1)}, f32[3,20,2,128]{3,2,1,0:T(2,128)S(1)}, u32[]{:S(2)}, u32[]{:S(2)}) collective-permute-start(f32[3,20,2,128]{3,2,1,0:T(2,128)S(1)} %get-tuple-element.432), channel_id=1, source_target_pairs={{1,0},{2,1},{3,2},{5,4},{6,5},{7,6},{9,8},{10,9},{11,10},{13,12},{... | collective-permute-start | bytes 184328 | tf_op jit(solution)/shard_map/ppermute | solution.py:22
  29.4 6.8 %collective-permute-start = (f32[1,4,3,16,128]{4,3,2,1,0:T(8,128)S(1)}, f32[1,4,3,16,128]{4,3,2,1,0:T(8,128)S(1)}, u32[]{:S(2)}, u32[]{:S(2)}) collective-permute-start(f32[1,4,3,16,128]{4,3,2,1,0:T(8,128)S(1)} %get-tuple-element.540), channel_id=1, source_target_pairs={{0,4},{4,8},{8,12},{12,16},{16,20},{20,24},{24,28},{1,5},{5,9},{9,... | collective-permute-start | bytes 294920 | tf_op jit(solution)/shard_map/while/body/eval_jaxpr/ppermute | solution.py:19
  33.9 6.5 %collective-permute-start.1 = (f32[1,4,3,16,128]{4,3,2,1,0:T(8,128)S(1)}, f32[1,4,3,16,128]{4,3,2,1,0:T(8,128)S(1)}, u32[]{:S(2)}, u32[]{:S(2)}) collective-permute-start(f32[1,4,3,16,128]{4,3,2,1,0:T(8,128)S(1)} %get-tuple-element.541), channel_id=1, source_target_pairs={{4,0},{8,4},{12,8},{16,12},{20,16},{24,20},{28,24},{5,1},{9,5},{13... | collective-permute-start | bytes 294920 | tf_op jit(solution)/shard_map/while/body/eval_jaxpr/ppermute | solution.py:22
  40.5 7.4 %collective-permute-start.2 = (f32[1,4,22,3,128]{4,3,2,1,0:T(4,128)S(1)}, f32[1,4,22,3,128]{4,3,2,1,0:T(4,128)S(1)}, u32[]{:S(2)}, u32[]{:S(2)}) collective-permute-start(f32[1,4,22,3,128]{4,3,2,1,0:T(4,128)S(1)} %get-tuple-element.542), channel_id=1, source_target_pairs={{1,0},{2,1},{3,2},{5,4},{6,5},{7,6},{9,8},{10,9},{11,10},{13,12},{... | collective-permute-start | bytes 405512 | tf_op jit(solution)/shard_map/while/body/eval_jaxpr/ppermute | solution.py:22
  43.0 7.4 %collective-permute-start.3 = (f32[1,4,22,3,128]{4,3,2,1,0:T(4,128)S(1)}, f32[1,4,22,3,128]{4,3,2,1,0:T(4,128)S(1)}, u32[]{:S(2)}, u32[]{:S(2)}) collective-permute-start(f32[1,4,22,3,128]{4,3,2,1,0:T(4,128)S(1)} %get-tuple-element.543), channel_id=1, source_target_pairs={{0,1},{1,2},{2,3},{4,5},{5,6},{6,7},{8,9},{9,10},{10,11},{12,13},{... | collective-permute-start | bytes 405512 | tf_op jit(solution)/shard_map/while/body/eval_jaxpr/ppermute | solution.py:19
  58.6 7.0 %collective-permute-start = (f32[1,4,3,16,128]{4,3,2,1,0:T(8,128)S(1)}, f32[1,4,3,16,128]{4,3,2,1,0:T(8,128)S(1)}, u32[]{:S(2)}, u32[]{:S(2)}) collective-permute-start(f32[1,4,3,16,128]{4,3,2,1,0:T(8,128)S(1)} %get-tuple-element.540), channel_id=1, source_target_pairs={{0,4},{4,8},{8,12},{12,16},{16,20},{20,24},{24,28},{1,5},{5,9},{9,... | collective-permute-start | bytes 294920 | tf_op jit(solution)/shard_map/while/body/eval_jaxpr/ppermute | solution.py:19
  63.4 7.7 %collective-permute-start.1 = (f32[1,4,3,16,128]{4,3,2,1,0:T(8,128)S(1)}, f32[1,4,3,16,128]{4,3,2,1,0:T(8,128)S(1)}, u32[]{:S(2)}, u32[]{:S(2)}) collective-permute-start(f32[1,4,3,16,128]{4,3,2,1,0:T(8,128)S(1)} %get-tuple-element.541), channel_id=1, source_target_pairs={{4,0},{8,4},{12,8},{16,12},{20,16},{24,20},{28,24},{5,1},{9,5},{13... | collective-permute-start | bytes 294920 | tf_op jit(solution)/shard_map/while/body/eval_jaxpr/ppermute | solution.py:22
  71.2 7.4 %collective-permute-start.2 = (f32[1,4,22,3,128]{4,3,2,1,0:T(4,128)S(1)}, f32[1,4,22,3,128]{4,3,2,1,0:T(4,128)S(1)}, u32[]{:S(2)}, u32[]{:S(2)}) collective-permute-start(f32[1,4,22,3,128]{4,3,2,1,0:T(4,128)S(1)} %get-tuple-element.542), channel_id=1, source_target_pairs={{1,0},{2,1},{3,2},{5,4},{6,5},{7,6},{9,8},{10,9},{11,10},{13,12},{... | collective-permute-start | bytes 405512 | tf_op jit(solution)/shard_map/while/body/eval_jaxpr/ppermute | solution.py:22
  73.2 7.4 %collective-permute-start.3 = (f32[1,4,22,3,128]{4,3,2,1,0:T(4,128)S(1)}, f32[1,4,22,3,128]{4,3,2,1,0:T(4,128)S(1)}, u32[]{:S(2)}, u32[]{:S(2)}) collective-permute-start(f32[1,4,22,3,128]{4,3,2,1,0:T(4,128)S(1)} %get-tuple-element.543), channel_id=1, source_target_pairs={{0,1},{1,2},{2,3},{4,5},{5,6},{6,7},{8,9},{9,10},{10,11},{12,13},{... | collective-permute-start | bytes 405512 | tf_op jit(solution)/shard_map/while/body/eval_jaxpr/ppermute | solution.py:19
  88.7 7.3 %collective-permute-start = (f32[1,4,3,16,128]{4,3,2,1,0:T(8,128)S(1)}, f32[1,4,3,16,128]{4,3,2,1,0:T(8,128)S(1)}, u32[]{:S(2)}, u32[]{:S(2)}) collective-permute-start(f32[1,4,3,16,128]{4,3,2,1,0:T(8,128)S(1)} %get-tuple-element.540), channel_id=1, source_target_pairs={{0,4},{4,8},{8,12},{12,16},{16,20},{20,24},{24,28},{1,5},{5,9},{9,... | collective-permute-start | bytes 294920 | tf_op jit(solution)/shard_map/while/body/eval_jaxpr/ppermute | solution.py:19
  93.9 6.5 %collective-permute-start.1 = (f32[1,4,3,16,128]{4,3,2,1,0:T(8,128)S(1)}, f32[1,4,3,16,128]{4,3,2,1,0:T(8,128)S(1)}, u32[]{:S(2)}, u32[]{:S(2)}) collective-permute-start(f32[1,4,3,16,128]{4,3,2,1,0:T(8,128)S(1)} %get-tuple-element.541), channel_id=1, source_target_pairs={{4,0},{8,4},{12,8},{16,12},{20,16},{24,20},{28,24},{5,1},{9,5},{13... | collective-permute-start | bytes 294920 | tf_op jit(solution)/shard_map/while/body/eval_jaxpr/ppermute | solution.py:22
  100.5 7.4 %collective-permute-start.2 = (f32[1,4,22,3,128]{4,3,2,1,0:T(4,128)S(1)}, f32[1,4,22,3,128]{4,3,2,1,0:T(4,128)S(1)}, u32[]{:S(2)}, u32[]{:S(2)}) collective-permute-start(f32[1,4,22,3,128]{4,3,2,1,0:T(4,128)S(1)} %get-tuple-element.542), channel_id=1, source_target_pairs={{1,0},{2,1},{3,2},{5,4},{6,5},{7,6},{9,8},{10,9},{11,10},{13,12},{... | collective-permute-start | bytes 405512 | tf_op jit(solution)/shard_map/while/body/eval_jaxpr/ppermute | solution.py:22
  102.4 7.4 %collective-permute-start.3 = (f32[1,4,22,3,128]{4,3,2,1,0:T(4,128)S(1)}, f32[1,4,22,3,128]{4,3,2,1,0:T(4,128)S(1)}, u32[]{:S(2)}, u32[]{:S(2)}) collective-permute-start(f32[1,4,22,3,128]{4,3,2,1,0:T(4,128)S(1)} %get-tuple-element.543), channel_id=1, source_target_pairs={{0,1},{1,2},{2,3},{4,5},{5,6},{6,7},{8,9},{9,10},{10,11},{12,13},{... | collective-permute-start | bytes 405512 | tf_op jit(solution)/shard_map/while/body/eval_jaxpr/ppermute | solution.py:19
  118.0 6.1 %collective-permute-start = (f32[1,4,3,16,128]{4,3,2,1,0:T(8,128)S(1)}, f32[1,4,3,16,128]{4,3,2,1,0:T(8,128)S(1)}, u32[]{:S(2)}, u32[]{:S(2)}) collective-permute-start(f32[1,4,3,16,128]{4,3,2,1,0:T(8,128)S(1)} %get-tuple-element.540), channel_id=1, source_target_pairs={{0,4},{4,8},{8,12},{12,16},{16,20},{20,24},{24,28},{1,5},{5,9},{9,... | collective-permute-start | bytes 294920 | tf_op jit(solution)/shard_map/while/body/eval_jaxpr/ppermute | solution.py:19
  121.9 6.5 %collective-permute-start.1 = (f32[1,4,3,16,128]{4,3,2,1,0:T(8,128)S(1)}, f32[1,4,3,16,128]{4,3,2,1,0:T(8,128)S(1)}, u32[]{:S(2)}, u32[]{:S(2)}) collective-permute-start(f32[1,4,3,16,128]{4,3,2,1,0:T(8,128)S(1)} %get-tuple-element.541), channel_id=1, source_target_pairs={{4,0},{8,4},{12,8},{16,12},{20,16},{24,20},{28,24},{5,1},{9,5},{13... | collective-permute-start | bytes 294920 | tf_op jit(solution)/shard_map/while/body/eval_jaxpr/ppermute | solution.py:22
  128.5 7.4 %collective-permute-start.2 = (f32[1,4,22,3,128]{4,3,2,1,0:T(4,128)S(1)}, f32[1,4,22,3,128]{4,3,2,1,0:T(4,128)S(1)}, u32[]{:S(2)}, u32[]{:S(2)}) collective-permute-start(f32[1,4,22,3,128]{4,3,2,1,0:T(4,128)S(1)} %get-tuple-element.542), channel_id=1, source_target_pairs={{1,0},{2,1},{3,2},{5,4},{6,5},{7,6},{9,8},{10,9},{11,10},{13,12},{... | collective-permute-start | bytes 405512 | tf_op jit(solution)/shard_map/while/body/eval_jaxpr/ppermute | solution.py:22
  130.4 7.4 %collective-permute-start.3 = (f32[1,4,22,3,128]{4,3,2,1,0:T(4,128)S(1)}, f32[1,4,22,3,128]{4,3,2,1,0:T(4,128)S(1)}, u32[]{:S(2)}, u32[]{:S(2)}) collective-permute-start(f32[1,4,22,3,128]{4,3,2,1,0:T(4,128)S(1)} %get-tuple-element.543), channel_id=1, source_target_pairs={{0,1},{1,2},{2,3},{4,5},{5,6},{6,7},{8,9},{9,10},{10,11},{12,13},{... | collective-permute-start | bytes 405512 | tf_op jit(solution)/shard_map/while/body/eval_jaxpr/ppermute | solution.py:19
  146.0 5.3 %collective-permute-start = (f32[1,4,3,16,128]{4,3,2,1,0:T(8,128)S(1)}, f32[1,4,3,16,128]{4,3,2,1,0:T(8,128)S(1)}, u32[]{:S(2)}, u32[]{:S(2)}) collective-permute-start(f32[1,4,3,16,128]{4,3,2,1,0:T(8,128)S(1)} %get-tuple-element.540), channel_id=1, source_target_pairs={{0,4},{4,8},{8,12},{12,16},{16,20},{20,24},{24,28},{1,5},{5,9},{9,... | collective-permute-start | bytes 294920 | tf_op jit(solution)/shard_map/while/body/eval_jaxpr/ppermute | solution.py:19
  149.1 6.5 %collective-permute-start.1 = (f32[1,4,3,16,128]{4,3,2,1,0:T(8,128)S(1)}, f32[1,4,3,16,128]{4,3,2,1,0:T(8,128)S(1)}, u32[]{:S(2)}, u32[]{:S(2)}) collective-permute-start(f32[1,4,3,16,128]{4,3,2,1,0:T(8,128)S(1)} %get-tuple-element.541), channel_id=1, source_target_pairs={{4,0},{8,4},{12,8},{16,12},{20,16},{24,20},{28,24},{5,1},{9,5},{13... | collective-permute-start | bytes 294920 | tf_op jit(solution)/shard_map/while/body/eval_jaxpr/ppermute | solution.py:22
  155.7 7.4 %collective-permute-start.2 = (f32[1,4,22,3,128]{4,3,2,1,0:T(4,128)S(1)}, f32[1,4,22,3,128]{4,3,2,1,0:T(4,128)S(1)}, u32[]{:S(2)}, u32[]{:S(2)}) collective-permute-start(f32[1,4,22,3,128]{4,3,2,1,0:T(4,128)S(1)} %get-tuple-element.542), channel_id=1, source_target_pairs={{1,0},{2,1},{3,2},{5,4},{6,5},{7,6},{9,8},{10,9},{11,10},{13,12},{... | collective-permute-start | bytes 405512 | tf_op jit(solution)/shard_map/while/body/eval_jaxpr/ppermute | solution.py:22
  157.7 7.4 %collective-permute-start.3 = (f32[1,4,22,3,128]{4,3,2,1,0:T(4,128)S(1)}, f32[1,4,22,3,128]{4,3,2,1,0:T(4,128)S(1)}, u32[]{:S(2)}, u32[]{:S(2)}) collective-permute-start(f32[1,4,22,3,128]{4,3,2,1,0:T(4,128)S(1)} %get-tuple-element.543), channel_id=1, source_target_pairs={{0,1},{1,2},{2,3},{4,5},{5,6},{6,7},{8,9},{9,10},{10,11},{12,13},{... | collective-permute-start | bytes 405512 | tf_op jit(solution)/shard_map/while/body/eval_jaxpr/ppermute | solution.py:19
  173.2 5.3 %collective-permute-start = (f32[1,4,3,16,128]{4,3,2,1,0:T(8,128)S(1)}, f32[1,4,3,16,128]{4,3,2,1,0:T(8,128)S(1)}, u32[]{:S(2)}, u32[]{:S(2)}) collective-permute-start(f32[1,4,3,16,128]{4,3,2,1,0:T(8,128)S(1)} %get-tuple-element.540), channel_id=1, source_target_pairs={{0,4},{4,8},{8,12},{12,16},{16,20},{20,24},{24,28},{1,5},{5,9},{9,... | collective-permute-start | bytes 294920 | tf_op jit(solution)/shard_map/while/body/eval_jaxpr/ppermute | solution.py:19
  176.4 6.5 %collective-permute-start.1 = (f32[1,4,3,16,128]{4,3,2,1,0:T(8,128)S(1)}, f32[1,4,3,16,128]{4,3,2,1,0:T(8,128)S(1)}, u32[]{:S(2)}, u32[]{:S(2)}) collective-permute-start(f32[1,4,3,16,128]{4,3,2,1,0:T(8,128)S(1)} %get-tuple-element.541), channel_id=1, source_target_pairs={{4,0},{8,4},{12,8},{16,12},{20,16},{24,20},{28,24},{5,1},{9,5},{13... | collective-permute-start | bytes 294920 | tf_op jit(solution)/shard_map/while/body/eval_jaxpr/ppermute | solution.py:22
  183.0 7.4 %collective-permute-start.2 = (f32[1,4,22,3,128]{4,3,2,1,0:T(4,128)S(1)}, f32[1,4,22,3,128]{4,3,2,1,0:T(4,128)S(1)}, u32[]{:S(2)}, u32[]{:S(2)}) collective-permute-start(f32[1,4,22,3,128]{4,3,2,1,0:T(4,128)S(1)} %get-tuple-element.542), channel_id=1, source_target_pairs={{1,0},{2,1},{3,2},{5,4},{6,5},{7,6},{9,8},{10,9},{11,10},{13,12},{... | collective-permute-start | bytes 405512 | tf_op jit(solution)/shard_map/while/body/eval_jaxpr/ppermute | solution.py:22
  184.9 7.4 %collective-permute-start.3 = (f32[1,4,22,3,128]{4,3,2,1,0:T(4,128)S(1)}, f32[1,4,22,3,128]{4,3,2,1,0:T(4,128)S(1)}, u32[]{:S(2)}, u32[]{:S(2)}) collective-permute-start(f32[1,4,22,3,128]{4,3,2,1,0:T(4,128)S(1)} %get-tuple-element.543), channel_id=1, source_target_pairs={{0,1},{1,2},{2,3},{4,5},{5,6},{6,7},{8,9},{9,10},{10,11},{12,13},{... | collective-permute-start | bytes 405512 | tf_op jit(solution)/shard_map/while/body/eval_jaxpr/ppermute | solution.py:19
  200.5 5.3 %collective-permute-start = (f32[1,4,3,16,128]{4,3,2,1,0:T(8,128)S(1)}, f32[1,4,3,16,128]{4,3,2,1,0:T(8,128)S(1)}, u32[]{:S(2)}, u32[]{:S(2)}) collective-permute-start(f32[1,4,3,16,128]{4,3,2,1,0:T(8,128)S(1)} %get-tuple-element.540), channel_id=1, source_target_pairs={{0,4},{4,8},{8,12},{12,16},{16,20},{20,24},{24,28},{1,5},{5,9},{9,... | collective-permute-start | bytes 294920 | tf_op jit(solution)/shard_map/while/body/eval_jaxpr/ppermute | solution.py:19
  203.6 6.5 %collective-permute-start.1 = (f32[1,4,3,16,128]{4,3,2,1,0:T(8,128)S(1)}, f32[1,4,3,16,128]{4,3,2,1,0:T(8,128)S(1)}, u32[]{:S(2)}, u32[]{:S(2)}) collective-permute-start(f32[1,4,3,16,128]{4,3,2,1,0:T(8,128)S(1)} %get-tuple-element.541), channel_id=1, source_target_pairs={{4,0},{8,4},{12,8},{16,12},{20,16},{24,20},{28,24},{5,1},{9,5},{13... | collective-permute-start | bytes 294920 | tf_op jit(solution)/shard_map/while/body/eval_jaxpr/ppermute | solution.py:22
  210.2 7.4 %collective-permute-start.2 = (f32[1,4,22,3,128]{4,3,2,1,0:T(4,128)S(1)}, f32[1,4,22,3,128]{4,3,2,1,0:T(4,128)S(1)}, u32[]{:S(2)}, u32[]{:S(2)}) collective-permute-start(f32[1,4,22,3,128]{4,3,2,1,0:T(4,128)S(1)} %get-tuple-element.542), channel_id=1, source_target_pairs={{1,0},{2,1},{3,2},{5,4},{6,5},{7,6},{9,8},{10,9},{11,10},{13,12},{... | collective-permute-start | bytes 405512 | tf_op jit(solution)/shard_map/while/body/eval_jaxpr/ppermute | solution.py:22
  212.1 7.4 %collective-permute-start.3 = (f32[1,4,22,3,128]{4,3,2,1,0:T(4,128)S(1)}, f32[1,4,22,3,128]{4,3,2,1,0:T(4,128)S(1)}, u32[]{:S(2)}, u32[]{:S(2)}) collective-permute-start(f32[1,4,22,3,128]{4,3,2,1,0:T(4,128)S(1)} %get-tuple-element.543), channel_id=1, source_target_pairs={{0,1},{1,2},{2,3},{4,5},{5,6},{6,7},{8,9},{9,10},{10,11},{12,13},{... | collective-permute-start | bytes 405512 | tf_op jit(solution)/shard_map/while/body/eval_jaxpr/ppermute | solution.py:19
  227.7 5.3 %collective-permute-start = (f32[1,4,3,16,128]{4,3,2,1,0:T(8,128)S(1)}, f32[1,4,3,16,128]{4,3,2,1,0:T(8,128)S(1)}, u32[]{:S(2)}, u32[]{:S(2)}) collective-permute-start(f32[1,4,3,16,128]{4,3,2,1,0:T(8,128)S(1)} %get-tuple-element.540), channel_id=1, source_target_pairs={{0,4},{4,8},{8,12},{12,16},{16,20},{20,24},{24,28},{1,5},{5,9},{9,... | collective-permute-start | bytes 294920 | tf_op jit(solution)/shard_map/while/body/eval_jaxpr/ppermute | solution.py:19
  230.8 6.5 %collective-permute-start.1 = (f32[1,4,3,16,128]{4,3,2,1,0:T(8,128)S(1)}, f32[1,4,3,16,128]{4,3,2,1,0:T(8,128)S(1)}, u32[]{:S(2)}, u32[]{:S(2)}) collective-permute-start(f32[1,4,3,16,128]{4,3,2,1,0:T(8,128)S(1)} %get-tuple-element.541), channel_id=1, source_target_pairs={{4,0},{8,4},{12,8},{16,12},{20,16},{24,20},{28,24},{5,1},{9,5},{13... | collective-permute-start | bytes 294920 | tf_op jit(solution)/shard_map/while/body/eval_jaxpr/ppermute | solution.py:22
  237.4 7.4 %collective-permute-start.2 = (f32[1,4,22,3,128]{4,3,2,1,0:T(4,128)S(1)}, f32[1,4,22,3,128]{4,3,2,1,0:T(4,128)S(1)}, u32[]{:S(2)}, u32[]{:S(2)}) collective-permute-start(f32[1,4,22,3,128]{4,3,2,1,0:T(4,128)S(1)} %get-tuple-element.542), channel_id=1, source_target_pairs={{1,0},{2,1},{3,2},{5,4},{6,5},{7,6},{9,8},{10,9},{11,10},{13,12},{... | collective-permute-start | bytes 405512 | tf_op jit(solution)/shard_map/while/body/eval_jaxpr/ppermute | solution.py:22
  239.4 7.4 %collective-permute-start.3 = (f32[1,4,22,3,128]{4,3,2,1,0:T(4,128)S(1)}, f32[1,4,22,3,128]{4,3,2,1,0:T(4,128)S(1)}, u32[]{:S(2)}, u32[]{:S(2)}) collective-permute-start(f32[1,4,22,3,128]{4,3,2,1,0:T(4,128)S(1)} %get-tuple-element.543), channel_id=1, source_target_pairs={{0,1},{1,2},{2,3},{4,5},{5,6},{6,7},{8,9},{9,10},{10,11},{12,13},{... | collective-permute-start | bytes 405512 | tf_op jit(solution)/shard_map/while/body/eval_jaxpr/ppermute | solution.py:19
  255.5 16.6 %all-to-all-start.1 = ((f32[32,1,8]{2,1,0:T(1,128)}), f32[32,1,8]{2,1,0:T(1,128)S(1)}, u32[]{:S(2)}, u32[]{:S(2)}) async-start(f32[32,1,8]{2,1,0:T(1,128)} %broadcast_in_dim.115), calls=%async_computation.1 | async-start | bytes 32768 | tf_op jit(solution)/shard_map/all_to_all | solution.py:35
where the time goes:
time: 274 us; the launch traced here: 273 us
  starting transfers between devices  112 us (41%)
  waiting for transfers between devices  86 us (31%)
  other arithmetic  57.8 us (21%)
  local copies, waits for them, and re-layouts  13.9 us (5%)
    ppermute x18, starting transfers between devices, padded_2(): lax.ppermute(lax.slice_in_dim(block, block.shape[dim] - width, None, axis...  69.1 us
    ppermute x18, waiting for transfers between devices, padded_2(): lax.ppermute(lax.slice_in_dim(block, 0, width, axis=dim), axis, backward)  50.5 us
    ppermute x18, starting transfers between devices, padded_2(): lax.ppermute(lax.slice_in_dim(block, 0, width, axis=dim), axis, backward)  30 us
    ppermute x18, waiting for transfers between devices, padded_2(): lax.ppermute(lax.slice_in_dim(block, block.shape[dim] - width, None, axis...  23.3 us
    broadcast_in_dim x8, other arithmetic, sweep(): return (jnp.concatenate([new_moved, new_damage[:, None]], axis=1), squares)  16.5 us
    all_to_all x2, starting transfers between devices, copy_for_each(): lax.all_to_all(jnp.broadcast_to(x[None], (length, *x.shape)), axis, 0, 0,...  12.6 us
    all_to_all x2, waiting for transfers between devices, copy_for_each(): lax.all_to_all(jnp.broadcast_to(x[None], (length, *x.shape)), axis, 0, 0,...  12.2 us
    mul x16, other arithmetic, elastic_parts(): jnp.expand_dims(face, -4) * (shifted(moved_pad, offset) - current)  8.87 us
  transfers between devices with their start and end apart: 38, of which 36 were waited for; matrix products, arithmetic and copies ran while one was open for 1% of the time, Pallas kernels for 0%

commit v1 on v0

v1 whole, which is shorter than its diff:
```python
import functools

import jax
import jax.numpy as jnp
from jax import lax
from jax.experimental import pallas as pl
from jax.experimental.pallas import tpu as pltpu
from jax.sharding import PartitionSpec as P

MESH = pl.DeviceIdType.MESH
relax_weight = 0.6
stiff_floor = 0.001
eigen_guard = 1e-08
outside_stiff = 1.001

cos_third = (
    0.8660254053677892, 0.166666399623719, -0.0481050217302989, 0.024608831949810825,
    -0.015124763172089219, 0.009420074574188678, -0.004972568153766589,
    0.0017909605462136829, -0.0003093201852607309,
)
sin_third = (
    0.49999999939158213, -0.038675031951822925, 0.015381770818675887, -0.00862700282428075,
    0.005525819902144846, -0.0035154216998851246, 0.0018763805597984632,
    -0.0006797757027300123, 0.00011778274999869613,
)

PITCH = 24
LEAD = 8
HALO = 2


def row_of(x, y):
    return (x + HALO) * PITCH + LEAD + y


def polynomial(coefficients, t):
    value = coefficients[-1]
    for coefficient in coefficients[-2::-1]:
        value = value * t + coefficient
    return value


def twice_energy(a, b, c, d, e, f):
    trace = a + b + c
    middle = trace * (1.0 / 3.0)
    a, b, c = a - middle, b - middle, c - middle
    dd, ee, ff = d * d, e * e, f * f
    spread = (a * a + b * b + c * c) * (1.0 / 6.0) + (dd + ee + ff) * (1.0 / 3.0)
    guarded = spread + 4.0 * eigen_guard
    determinant = a * (b * c - ff) - d * (d * c - f * e) + e * (d * f - b * e)
    inverse = lax.rsqrt(guarded)
    ratio = determinant * (0.5 * inverse) * (inverse * inverse)
    size = jnp.minimum(jnp.abs(ratio), 1.0)
    radius = jnp.sqrt(spread)
    first = radius * polynomial(cos_third, size)
    first = jnp.where(ratio < 0.0, -first, first)
    rest = radius * (1.7320508075688772 * jnp.sqrt(1.0 - size)) * polynomial(sin_third, size)
    largest = jnp.maximum(middle + 2.0 * first, 0.0)
    base = middle - first
    second = jnp.maximum(base + rest, 0.0)
    third = jnp.maximum(base - rest, 0.0)
    volume = jnp.maximum(trace, 0.0)
    energy = 0.25 * (volume * volume) + 0.5 * (
        largest * largest + second * second + third * third
    )
    return energy, trace


def kernel(
    sizes, bx, by, cells,
    index_ref, loads_ref, tough_ref, clamp_ref, load_ref, crack_ref,
    disp_ref, dam_ref, table_ref,
    u, df, kk, lf, clamp_v, load_v, crack_v, g,
    pa, ra, pb, rb, pc, rc, row_v, rows_v,
    local_sem, a_send, a_recv, b_send, b_recv, t_send, t_recv, s_send, s_recv,
):
    ns, nx, ny = sizes
    me_s = lax.axis_index("section")
    me_x = lax.axis_index("gx")
    me_y = lax.axis_index("gy")
    nz = u.shape[-1]
    rows = u.shape[1]

    copies = [
        pltpu.make_async_copy(source, target, local_sem.at[i])
        for i, (source, target) in enumerate(
            ((load_ref, load_v), (clamp_ref, clamp_v), (crack_ref, crack_v), (tough_ref, g.at[0]))
        )
    ]
    for copy in copies:
        copy.start()

    halo_pieces = [(i * PITCH, 8) for i in range(bx + 2 * HALO + 1)]
    halo_pieces += [(row_of(x, 0), by) for x in (-2, -1, bx, bx + 1)]
    for start, size in halo_pieces:
        for i in range(u.shape[0]):
            u[i, pl.ds(start, size), :] = jnp.zeros((size, nz), jnp.float32)
        for i in range(df.shape[0]):
            df[i, pl.ds(start, size), :] = jnp.zeros((size, nz), jnp.float32)
        lf[0, pl.ds(start, size), :] = jnp.zeros((size, nz), jnp.float32)
        lf[1, pl.ds(start, size), :] = jnp.ones((size, nz), jnp.float32)
        kk[pl.ds(start, size), :] = jnp.full((size, nz), outside_stiff, jnp.float32)

    def there(dx, dy):
        return (
            (me_x + dx >= 0) & (me_x + dx < nx) & (me_y + dy >= 0) & (me_y + dy < ny)
        )

    corners = ((-1, -1), (-1, 1), (1, -1), (1, 1))
    sides_x = ((-1, 0), (1, 0))
    sides_y = ((0, -1), (0, 1))
    neighbours = sides_x + sides_y + corners

    barrier = pltpu.get_barrier_semaphore()
    for dx, dy in neighbours:
        @pl.when(there(dx, dy))
        def _(dx=dx, dy=dy):
            pl.semaphore_signal(
                barrier, inc=1, device_id={"gx": me_x + dx, "gy": me_y + dy}, device_id_type=MESH
            )
    for r in range(1, ns):
        pl.semaphore_signal(
            barrier, inc=1, device_id={"section": lax.rem(me_s + r, ns)}, device_id_type=MESH
        )

    for i in (0, 1, 2):
        copies[i].wait()

    def begin(x, carry):
        here = pl.ds(row_of(x, 0), by)
        held = pl.ds(x * by, by)
        load = load_v[held, :].astype(jnp.float32)
        clamp = clamp_v[held, :].astype(jnp.float32)
        crack = crack_v[held, :].astype(jnp.float32)
        lf[0, here, :] = load
        lf[1, here, :] = jnp.maximum(load, clamp)
        df[0, here, :] = crack
        kk[here, :] = (1.0 - crack) * (1.0 - crack) + stiff_floor
        return carry

    lax.fori_loop(0, bx, begin, 0, unroll=4)

    across = 1 + (me_x > 0).astype(jnp.int32) + (me_x < nx - 1).astype(jnp.int32)
    along = 1 + (me_y > 0).astype(jnp.int32) + (me_y < ny - 1).astype(jnp.int32)
    pl.semaphore_wait(barrier, across * along - 1 + (ns - 1))

    def remote(source, target, send, recv, dx, dy):
        return pltpu.make_async_remote_copy(
            src_ref=source, dst_ref=target, send_sem=send, recv_sem=recv,
            device_id={"gx": me_x + dx, "gy": me_y + dy}, device_id_type=MESH,
        )

    def b_copies(field, base, q, dx, dy):
        found = []
        if dy == 0:
            for layer in range(HALO):
                x = layer if dx < 0 else bx - HALO + layer
                to = bx + layer if dx < 0 else layer - HALO
                i = (0 if dx < 0 else 2) + layer
                found.append(remote(
                    field.at[pl.ds(base, 2), pl.ds(row_of(x, 0), by), :],
                    field.at[pl.ds(base, 2), pl.ds(row_of(to, 0), by), :],
                    b_send.at[q, i], b_recv.at[q, i], dx, dy,
                ))
        elif dx == 0:
            i = 0 if dy < 0 else 1
            found.append(remote(
                pb.at[i], rb.at[q, i], b_send.at[q, 4 + i], b_recv.at[q, 4 + i], dx, dy,
            ))
        else:
            i = corners.index((dx, dy))
            found.append(remote(
                pc.at[i], rc.at[q, i], b_send.at[q, 6 + i], b_recv.at[q, 6 + i], dx, dy,
            ))
        return found

    order_b = corners + sides_x + sides_y

    def send_b(field, base, q, current):
        for i, (dx, dy) in enumerate(corners):
            row = row_of(0 if dx < 0 else bx - 1, 0 if dy < 0 else by - 1)
            if current is not None:
                for c in range(3):
                    pc[i, pl.ds(c, 1), :] = u[current * 3 + c, pl.ds(row, 1), :]
            for f in range(2):
                pc[i, pl.ds(3 + f, 1), :] = field[base + f, pl.ds(row, 1), :]
        for i in range(2):
            for f in range(2):
                for layer in range(HALO):
                    y = layer if i == 0 else by - HALO + layer
                    pb[i, f * HALO + layer] = field[
                        base + f, pl.ds(row_of(0, y), bx, stride=PITCH), :
                    ]
        for dx, dy in order_b:
            @pl.when(there(dx, dy))
            def _(dx=dx, dy=dy):
                for copy in b_copies(field, base, q, dx, dy):
                    copy.start()

    def sent_b(field, base, q):
        for dx, dy in order_b:
            @pl.when(there(dx, dy))
            def _(dx=dx, dy=dy):
                for copy in b_copies(field, base, q, dx, dy):
                    copy.wait_send()

    def take_b(field, base, q, current):
        for dx, dy in order_b:
            @pl.when(there(-dx, -dy))
            def _(dx=dx, dy=dy):
                for copy in b_copies(field, base, q, dx, dy):
                    copy.wait_recv()
                if dx == 0:
                    i = 0 if dy < 0 else 1
                    for f in range(2):
                        for layer in range(HALO):
                            y = by + layer if i == 0 else layer - HALO
                            strip = pl.ds(row_of(0, y), bx, stride=PITCH)
                            value = rb[q, i, f * HALO + layer]
                            field[base + f, strip, :] = value
                            if current is not None and f == 0:
                                kk[strip, :] = (1.0 - value) * (1.0 - value) + stiff_floor
                elif dy != 0:
                    i = corners.index((dx, dy))
                    row = row_of(bx if dx < 0 else -1, by if dy < 0 else -1)
                    if current is not None:
                        for c in range(3):
                            u[current * 3 + c, pl.ds(row, 1), :] = rc[q, i, pl.ds(c, 1), :]
                        value = rc[q, i, pl.ds(3, 1), :]
                        kk[pl.ds(row, 1), :] = (1.0 - value) * (1.0 - value) + stiff_floor
                    for f in range(2):
                        field[base + f, pl.ds(row, 1), :] = rc[q, i, pl.ds(3 + f, 1), :]
        if current is not None:
            for x in (-2, -1, bx, bx + 1):
                here = pl.ds(row_of(x, 0), by)
                value = field[base, here, :]
                kk[here, :] = (1.0 - value) * (1.0 - value) + stiff_floor

    def a_copy(q, dx, dy):
        if dy == 0:
            i = 0 if dx < 0 else 1
            x, to = (1, bx + 1) if dx < 0 else (bx - 2, -2)
            return remote(
                u.at[pl.ds(q * 3, 3), pl.ds(row_of(x, 0), by), :],
                u.at[pl.ds(q * 3, 3), pl.ds(row_of(to, 0), by), :],
                a_send.at[q, i], a_recv.at[q, i], dx, dy,
            )
        i = 0 if dy < 0 else 1
        return remote(
            pa.at[i], ra.at[q, i], a_send.at[q, 2 + i], a_recv.at[q, 2 + i], dx, dy,
        )

    def send_a(q):
        for i in range(2):
            y = 1 if i == 0 else by - 2
            for c in range(3):
                pa[i, c] = u[q * 3 + c, pl.ds(row_of(0, y), bx, stride=PITCH), :]
        for dx, dy in sides_x + sides_y:
            @pl.when(there(dx, dy))
            def _(dx=dx, dy=dy):
                a_copy(q, dx, dy).start()

    def sent_a(q):
        for dx, dy in sides_x + sides_y:
            @pl.when(there(dx, dy))
            def _(dx=dx, dy=dy):
                a_copy(q, dx, dy).wait_send()

    def take_a(q):
        for dx, dy in sides_x + sides_y:
            @pl.when(there(-dx, -dy))
            def _(dx=dx, dy=dy):
                a_copy(q, dx, dy).wait_recv()
                if dx == 0:
                    i = 0 if dy < 0 else 1
                    y = by + 1 if i == 0 else -2
                    for c in range(3):
                        u[q * 3 + c, pl.ds(row_of(0, y), bx, stride=PITCH), :] = ra[q, i, c]

    def tough_copy(r):
        return pltpu.make_async_remote_copy(
            src_ref=tough_ref, dst_ref=g.at[r], send_sem=t_send.at[r], recv_sem=t_recv.at[r],
            device_id={"section": lax.rem(me_s + ns - r, ns)}, device_id_type=MESH,
        )

    send_b(lf, 0, 1, None)
    for r in range(1, ns):
        tough_copy(r).start()

    lane = lax.broadcasted_iota(jnp.int32, (by, nz), 1)
    at_low = lane == 0
    at_high = lane == nz - 1

    def from_low(value, edge):
        return jnp.where(at_low, edge, pltpu.roll(value, 1, 1))

    def from_high(value, edge):
        return jnp.where(at_high, edge, pltpu.roll(value, nz - 1, 1))

    def span(start, stride):
        return pl.ds(start, by) if stride == 1 else pl.ds(start, bx, stride=stride)

    case = index_ref[0]
    vector = [loads_ref[case, c] for c in range(3)]

    take_b(lf, 0, 1, None)

    def fill(x, carry):
        here = pl.ds(x * PITCH, PITCH)
        load = lf[0, here, :]
        for c in range(3):
            u[c, here, :] = load * vector[c]
        return carry

    lax.fori_loop(0, bx + 2 * HALO, fill, 0, unroll=2)
    tail = pl.ds((bx + 2 * HALO) * PITCH, 8)
    for c in range(3):
        u[c, tail, :] = lf[0, tail, :] * vector[c]

    def first_flow(x, carry):
        start = row_of(x, 0)
        trace = (
            u[0, pl.ds(start + PITCH, by), :] - u[0, pl.ds(start - PITCH, by), :]
            + u[1, pl.ds(start + 1, by), :] - u[1, pl.ds(start - 1, by), :]
        )
        value = u[2, pl.ds(start, by), :]
        trace = trace + (from_high(value, 0.0) - from_low(value, 0.0))
        df[1, pl.ds(start, by), :] = kk[pl.ds(start, by), :] * (0.5 * trace)
        return carry

    lax.fori_loop(0, bx, first_flow, 0, unroll=4)
    sent_b(lf, 0, 1)
    send_b(df, 0, 0, 0)
    copies[3].wait()

    def move(p, start, stride, out_x=None):
        q = 1 - p
        def at(ref, offset, *lead):
            return ref[(*lead, span(start + offset, stride), slice(None))]

        k = at(kk, 0)
        k_xm, k_xp = at(kk, -PITCH), at(kk, PITCH)
        k_ym, k_yp = at(kk, -1), at(kk, 1)
        k_zm, k_zp = from_low(k, outside_stiff), from_high(k, outside_stiff)
        pairs = (k_xm + k_xp, k_ym + k_yp, k_zm + k_zp)
        total = 6.0 * k + (pairs[0] + pairs[1] + pairs[2])
        w_xm, w_xp, w_ym, w_yp = k + k_xm, k + k_xp, k + k_ym, k + k_yp
        w_zm = jnp.where(at_low, 0.0, k + k_zm)
        w_zp = jnp.where(at_high, 0.0, k + k_zp)
        flow = 2 * p + 1
        middle_flow = at(df, 0, flow)
        slopes = (
            at(df, PITCH, flow) - at(df, -PITCH, flow),
            at(df, 1, flow) - at(df, -1, flow),
            from_high(middle_flow, 0.0) - from_low(middle_flow, 0.0),
        )
        fixed = at(lf, 0, 1) > 0.5
        load = at(lf, 0, 0)
        squares = None
        for c in range(3):
            f = p * 3 + c
            here = at(u, 0, f)
            total_c = (
                w_xm * at(u, -PITCH, f) + w_xp * at(u, PITCH, f)
                + w_ym * at(u, -1, f) + w_yp * at(u, 1, f)
                + w_zm * pltpu.roll(here, 1, 1) + w_zp * pltpu.roll(here, nz - 1, 1)
            )
            residual = total_c - total * here + 2.0 * slopes[c]
            relaxed = here + relax_weight * residual / (total + pairs[c])
            new = jnp.where(fixed, load * vector[c], relaxed)
            u[q * 3 + c, span(start, stride), :] = new
            if out_x is not None and out_x[0]:
                disp_ref[0, c, out_x[1]] = new
            square = residual * residual
            squares = square if squares is None else squares + square
        return jnp.where(fixed, 0.0, squares)

    def heal(p, r, x, last):
        q = 1 - p
        start = row_of(x, 0)
        def at(offset, f):
            return u[f, pl.ds(start + offset, by), :]

        grads = []
        for c in range(3):
            f = q * 3 + c
            here = at(0, f)
            grads.append((
                at(PITCH, f) - at(-PITCH, f),
                at(1, f) - at(-1, f),
                from_high(here, 0.0) - from_low(here, 0.0),
            ))
        energy, trace = twice_energy(
            grads[0][0], grads[1][1], grads[2][2],
            0.5 * (grads[0][1] + grads[1][0]),
            0.5 * (grads[0][2] + grads[2][0]),
            0.5 * (grads[1][2] + grads[2][1]),
        )
        def near(offset):
            return df[2 * p, pl.ds(start + offset, by), :]

        here = near(0)
        beside = (
            near(PITCH) + near(-PITCH) + near(1) + near(-1)
            + from_high(here, 0.0) + from_low(here, 0.0)
        )
        held = pl.ds(x * by, by)
        rate = g[r, held, :]
        renewed = (energy + rate * beside) / (energy + 7.0 * rate)
        renewed = jnp.where(crack_v[held, :] > 0, 1.0, renewed)
        if last:
            dam_ref[0, x] = renewed
        else:
            stiff = (1.0 - renewed) * (1.0 - renewed) + stiff_floor
            df[2 * q, pl.ds(start, by), :] = renewed
            kk[pl.ds(start, by), :] = stiff
            df[2 * q + 1, pl.ds(start, by), :] = stiff * (0.5 * trace)

    columns = lax.broadcasted_iota(jnp.int32, (1, nz), 1)

    def sweep(r, table, last):
        p = lax.rem(r, 2)
        q = 1 - p
        take_b(df, 2 * p, p, p)

        def move_own(x, total):
            return total + move(p, row_of(x, 0), 1, (last, x))

        squares = lax.fori_loop(
            0, bx, move_own, jnp.zeros((by, nz), jnp.float32), unroll=4
        )
        if not last:
            @pl.when(r > 0)
            def _():
                sent_a(p)
            send_a(q)
        else:
            sent_a(p)
        total = jnp.sum(jnp.sum(squares, axis=0, keepdims=True), axis=1, keepdims=True)
        column = lax.rem(me_s + r, ns)
        table = jnp.where(columns == column, jnp.broadcast_to(total, (1, nz)), table)
        if last:
            spread_sums(table)
        for x in (-1, bx):
            move(p, row_of(x, 0), 1)
        for y in (-1, by):
            move(p, row_of(0, y), PITCH)

        if last:
            tough_copy(r).wait_recv()
        else:
            @pl.when(r > 0)
            def _():
                tough_copy(r).wait_recv()

        def heal_own(x, carry):
            heal(p, r, x, last)
            return carry

        lax.fori_loop(0, bx, heal_own, 0, unroll=4)
        sent_b(df, 2 * p, p)
        if not last:
            send_b(df, 2 * q, q, q)
            take_a(q)
        return table

    def sums_copy(t):
        me = me_x * ny + me_y
        to = lax.rem(me + t, nx * ny)
        return pltpu.make_async_remote_copy(
            src_ref=row_v, dst_ref=rows_v.at[me], send_sem=s_send.at[t], recv_sem=s_recv.at[t],
            device_id={"gx": to // ny, "gy": lax.rem(to, ny)}, device_id_type=MESH,
        )

    def from_copy(t):
        me = me_x * ny + me_y
        source = lax.rem(me + nx * ny - t, nx * ny)
        return pltpu.make_async_remote_copy(
            src_ref=row_v, dst_ref=rows_v.at[source], send_sem=s_send.at[t], recv_sem=s_recv.at[t],
            device_id={"gx": me_x, "gy": me_y}, device_id_type=MESH,
        )

    def spread_sums(table):
        row_v[...] = table
        rows_v[me_x * ny + me_y] = table

        def start(t, carry):
            sums_copy(t).start()
            return carry

        lax.fori_loop(1, nx * ny, start, 0)

    table = lax.fori_loop(
        0, ns - 1, lambda r, t: sweep(r, t, False), jnp.zeros((1, nz), jnp.float32)
    )
    sweep(jnp.int32(ns - 1), table, True)

    for r in range(1, ns):
        tough_copy(r).wait_send()

    def finish(t, carry):
        sums_copy(t).wait_send()
        from_copy(t).wait_recv()
        return carry

    lax.fori_loop(1, nx * ny, finish, 0)
    everything = rows_v[0]
    for i in range(1, nx * ny):
        everything = everything + rows_v[i]
    result = jnp.sqrt(everything * (0.25 / (3.0 * cells)))
    table_ref[...] = result[:, :ns]


def on_device(sizes, load_index, load_table, toughness, clamp_mask, load_mask, crack_mask):
    ns, nx, ny = sizes
    bx, by, nz = clamp_mask.shape
    cells = float(clamp_mask.size * nx * ny)
    rows = (bx + 2 * HALO) * PITCH + LEAD
    flat = (bx * by, nz)
    f32 = jnp.float32
    scratch = [
        pltpu.VMEM((6, rows, nz), f32),
        pltpu.VMEM((4, rows, nz), f32),
        pltpu.VMEM((rows, nz), f32),
        pltpu.VMEM((2, rows, nz), f32),
        pltpu.VMEM(flat, jnp.int32),
        pltpu.VMEM(flat, jnp.int32),
        pltpu.VMEM(flat, jnp.int32),
        pltpu.VMEM((ns, *flat), f32),
        pltpu.VMEM((2, 3, bx, nz), f32),
        pltpu.VMEM((2, 2, 3, bx, nz), f32),
        pltpu.VMEM((2, 2 * HALO, bx, nz), f32),
        pltpu.VMEM((2, 2, 2 * HALO, bx, nz), f32),
        pltpu.VMEM((4, 8, nz), f32),
        pltpu.VMEM((2, 4, 8, nz), f32),
        pltpu.VMEM((1, nz), f32),
        pltpu.VMEM((nx * ny, 1, nz), f32),
        pltpu.SemaphoreType.DMA((4,)),
        pltpu.SemaphoreType.DMA((2, 4)),
        pltpu.SemaphoreType.DMA((2, 4)),
        pltpu.SemaphoreType.DMA((2, 10)),
        pltpu.SemaphoreType.DMA((2, 10)),
        pltpu.SemaphoreType.DMA((ns,)),
        pltpu.SemaphoreType.DMA((ns,)),
        pltpu.SemaphoreType.DMA((nx * ny,)),
        pltpu.SemaphoreType.DMA((nx * ny,)),
    ]
    smem = pl.BlockSpec(memory_space=pltpu.SMEM)
    vmem = pl.BlockSpec(memory_space=pltpu.VMEM)
    hbm = pl.BlockSpec(memory_space=pl.ANY)
    return pl.pallas_call(
        functools.partial(kernel, sizes, bx, by, cells),
        out_shape=(
            jax.ShapeDtypeStruct((1, 3, bx, by, nz), f32),
            jax.ShapeDtypeStruct((1, bx, by, nz), f32),
            jax.ShapeDtypeStruct((1, ns), f32),
        ),
        in_specs=[smem, smem, hbm, hbm, hbm, hbm],
        out_specs=(vmem, vmem, vmem),
        scratch_shapes=scratch,
        compiler_params=pltpu.CompilerParams(collective_id=0, has_side_effects=True),
        name="sweeps",
    )(
        load_index,
        load_table,
        toughness.reshape(flat),
        clamp_mask.reshape(flat),
        load_mask.reshape(flat),
        crack_mask.reshape(flat),
    )


def solution(mesh):
    sizes = (mesh.shape["section"], mesh.shape["gx"], mesh.shape["gy"])
    in_specs = (
        P("section"),
        P(),
        P("section", "gx", "gy", None),
        P("gx", "gy", None),
        P("gx", "gy", None),
        P("gx", "gy", None),
    )
    out_specs = (
        P("section", None, "gx", "gy", None),
        P("section", "gx", "gy", None),
        P("section", None),
    )
    return jax.shard_map(
        functools.partial(on_device, sizes),
        mesh=mesh, in_specs=in_specs, out_specs=out_specs, check_vma=False,
    )
```

time: 274 us -> 98.1 us (0.36)
  the two profiles are of different devices: /device:TPU:2 before, /device:TPU:16 now
where the time goes in v1:
time: 98.1 us; the launch traced here: 97.8 us
  Pallas kernels  92.2 us (94%)
  local copies, waits for them, and re-layouts  4.36 us (4%)
  between operations  1.3 us (1%)
    pallas_call x1, Pallas kernels, on_device(): pl.pallas_call(functools.partial(kernel, sizes, bx, by, cells), out_shape...  92.2 us
    unnamed x10, local copies, waits for them, and re-layouts  4.36 us

profile of v1, /device:TPU:16, one launch (start us, length us, event | category | flops | bytes accessed | tf_op | source)
XLA Modules:
  0.0 97.8 jit_solution(1312520785484103195)
XLA Ops:
  1.3 0.0 copy-start.1
  1.3 0.7 copy-done.1
  2.0 0.7 copy.9.loads_ref
  2.7 92.2 %sweeps.1 = (f32[1,3,16,16,128]{4,3,2,1,0:T(8,128)}, f32[1,16,16,128]{3,2,1,0:T(8,128)}, f32[1,8]{1,0:T(1,128)}) custom-call(s32[1]{0:T(128)S(6)} %copy.13.index_ref, f32[64,3]{1,0:T(8,128)} %copy.9.loads_ref, f32[256,128]{1,0:T(8,128)} %bitcast.4, s32[256,128]{1,0:T(8,128)} %bitcast.5, s32[256,128]{1,0:T(8,128)} %bitcast.6, s32[256,128]{1,0:T(8,128)} %bitcast.7), custom_call_target="tpu_custom_call" | custom-call | tf_op jit(solution)/shard_map/sweeps/pallas_call | solution.py:551
  94.8 0.0 copy-start
  94.8 1.8 %copy.14 = f32[1,3,16,16,128]{4,3,2,1,0:T(8,128)} copy(f32[1,3,16,16,128]{4,3,2,1,0:T(8,128)} %get-tuple-element.6) | data formatting | bytes 786432
  96.6 0.0 copy-done
  96.6 0.0 copy-start.2
  96.7 0.7 copy.15
  97.3 0.0 copy-done.2
  97.3 0.5 copy.16
Async XLA Ops:
  1.3 0.7 copy-start.1
  94.8 1.8 %copy-start = (f32[1,16,16,128]{3,2,1,0:T(8,128)S(1)}, f32[1,16,16,128]{3,2,1,0:T(8,128)}, u32[]{:S(2)}) copy-start(f32[1,16,16,128]{3,2,1,0:T(8,128)} %get-tuple-element.7) | copy-start | bytes 393220
  96.6 0.7 copy-start.2

commit v2 on v1

--- a/solution.py
+++ b/solution.py
@@ -27,6 +27,7 @@
 PITCH = 24
 LEAD = 8
 HALO = 2
+group = 8
 
 
 def row_of(x, y):
@@ -70,7 +71,7 @@
     sizes, bx, by, cells,
     index_ref, loads_ref, tough_ref, clamp_ref, load_ref, crack_ref,
     disp_ref, dam_ref, table_ref,
-    u, df, kk, lf, clamp_v, load_v, crack_v, g,
+    u0, u1, df0, df1, kk, lf, clamp_v, load_v, crack_v, g,
     pa, ra, pb, rb, pc, rc, row_v, rows_v,
     local_sem, a_send, a_recv, b_send, b_recv, t_send, t_recv, s_send, s_recv,
 ):
@@ -78,8 +79,8 @@
     me_s = lax.axis_index("section")
     me_x = lax.axis_index("gx")
     me_y = lax.axis_index("gy")
-    nz = u.shape[-1]
-    rows = u.shape[1]
+    nz = u0.shape[-1]
+    us, dfs = (u0, u1), (df0, df1)
 
     copies = [
         pltpu.make_async_copy(source, target, local_sem.at[i])
@@ -93,10 +94,9 @@
     halo_pieces = [(i * PITCH, 8) for i in range(bx + 2 * HALO + 1)]
     halo_pieces += [(row_of(x, 0), by) for x in (-2, -1, bx, bx + 1)]
     for start, size in halo_pieces:
-        for i in range(u.shape[0]):
-            u[i, pl.ds(start, size), :] = jnp.zeros((size, nz), jnp.float32)
-        for i in range(df.shape[0]):
-            df[i, pl.ds(start, size), :] = jnp.zeros((size, nz), jnp.float32)
+        for ref in us + dfs:
+            for i in range(ref.shape[0]):
+                ref[i, pl.ds(start, size), :] = jnp.zeros((size, nz), jnp.float32)
         lf[0, pl.ds(start, size), :] = jnp.zeros((size, nz), jnp.float32)
         lf[1, pl.ds(start, size), :] = jnp.ones((size, nz), jnp.float32)
         kk[pl.ds(start, size), :] = jnp.full((size, nz), outside_stiff, jnp.float32)
@@ -134,7 +134,7 @@
         crack = crack_v[held, :].astype(jnp.float32)
         lf[0, here, :] = load
         lf[1, here, :] = jnp.maximum(load, clamp)
-        df[0, here, :] = crack
+        df0[0, here, :] = crack
         kk[here, :] = (1.0 - crack) * (1.0 - crack) + stiff_floor
         return carry
 
@@ -150,7 +150,7 @@
             device_id={"gx": me_x + dx, "gy": me_y + dy}, device_id_type=MESH,
         )
 
-    def b_copies(field, base, q, dx, dy):
+    def b_copies(field, q, dx, dy):
         found = []
         if dy == 0:
             for layer in range(HALO):
@@ -158,8 +158,8 @@
                 to = bx + layer if dx < 0 else layer - HALO
                 i = (0 if dx < 0 else 2) + layer
                 found.append(remote(
-                    field.at[pl.ds(base, 2), pl.ds(row_of(x, 0), by), :],
-                    field.at[pl.ds(base, 2), pl.ds(row_of(to, 0), by), :],
+                    field.at[:, pl.ds(row_of(x, 0), by), :],
+                    field.at[:, pl.ds(row_of(to, 0), by), :],
                     b_send.at[q, i], b_recv.at[q, i], dx, dy,
                 ))
         elif dx == 0:
@@ -176,39 +176,39 @@
 
     order_b = corners + sides_x + sides_y
 
-    def send_b(field, base, q, current):
+    def send_b(field, q, current):
         for i, (dx, dy) in enumerate(corners):
             row = row_of(0 if dx < 0 else bx - 1, 0 if dy < 0 else by - 1)
             if current is not None:
                 for c in range(3):
-                    pc[i, pl.ds(c, 1), :] = u[current * 3 + c, pl.ds(row, 1), :]
+                    pc[i, pl.ds(c, 1), :] = current[c, pl.ds(row, 1), :]
             for f in range(2):
-                pc[i, pl.ds(3 + f, 1), :] = field[base + f, pl.ds(row, 1), :]
+                pc[i, pl.ds(3 + f, 1), :] = field[f, pl.ds(row, 1), :]
         for i in range(2):
             for f in range(2):
                 for layer in range(HALO):
                     y = layer if i == 0 else by - HALO + layer
                     pb[i, f * HALO + layer] = field[
-                        base + f, pl.ds(row_of(0, y), bx, stride=PITCH), :
+                        f, pl.ds(row_of(0, y), bx, stride=PITCH), :
                     ]
         for dx, dy in order_b:
             @pl.when(there(dx, dy))
             def _(dx=dx, dy=dy):
-                for copy in b_copies(field, base, q, dx, dy):
+                for copy in b_copies(field, q, dx, dy):
                     copy.start()
 
-    def sent_b(field, base, q):
+    def sent_b(field, q):
         for dx, dy in order_b:
             @pl.when(there(dx, dy))
             def _(dx=dx, dy=dy):
-                for copy in b_copies(field, base, q, dx, dy):
+                for copy in b_copies(field, q, dx, dy):
                     copy.wait_send()
 
-    def take_b(field, base, q, current):
+    def take_b(field, q, current):
         for dx, dy in order_b:
             @pl.when(there(-dx, -dy))
             def _(dx=dx, dy=dy):
-                for copy in b_copies(field, base, q, dx, dy):
+                for copy in b_copies(field, q, dx, dy):
                     copy.wait_recv()
                 if dx == 0:
                     i = 0 if dy < 0 else 1
@@ -217,7 +217,7 @@
                             y = by + layer if i == 0 else layer - HALO
                             strip = pl.ds(row_of(0, y), bx, stride=PITCH)
                             value = rb[q, i, f * HALO + layer]
-                            field[base + f, strip, :] = value
+                            field[f, strip, :] = value
                             if current is not None and f == 0:
                                 kk[strip, :] = (1.0 - value) * (1.0 - value) + stiff_floor
                 elif dy != 0:
@@ -225,15 +225,15 @@
                     row = row_of(bx if dx < 0 else -1, by if dy < 0 else -1)
                     if current is not None:
                         for c in range(3):
-                            u[current * 3 + c, pl.ds(row, 1), :] = rc[q, i, pl.ds(c, 1), :]
+                            current[c, pl.ds(row, 1), :] = rc[q, i, pl.ds(c, 1), :]
                         value = rc[q, i, pl.ds(3, 1), :]
                         kk[pl.ds(row, 1), :] = (1.0 - value) * (1.0 - value) + stiff_floor
                     for f in range(2):
-                        field[base + f, pl.ds(row, 1), :] = rc[q, i, pl.ds(3 + f, 1), :]
+                        field[f, pl.ds(row, 1), :] = rc[q, i, pl.ds(3 + f, 1), :]
         if current is not None:
             for x in (-2, -1, bx, bx + 1):
                 here = pl.ds(row_of(x, 0), by)
-                value = field[base, here, :]
+                value = field[0, here, :]
                 kk[here, :] = (1.0 - value) * (1.0 - value) + stiff_floor
 
     def a_copy(q, dx, dy):
@@ -241,8 +241,8 @@
             i = 0 if dx < 0 else 1
             x, to = (1, bx + 1) if dx < 0 else (bx - 2, -2)
             return remote(
-                u.at[pl.ds(q * 3, 3), pl.ds(row_of(x, 0), by), :],
-                u.at[pl.ds(q * 3, 3), pl.ds(row_of(to, 0), by), :],
+                us[q].at[:, pl.ds(row_of(x, 0), by), :],
+                us[q].at[:, pl.ds(row_of(to, 0), by), :],
                 a_send.at[q, i], a_recv.at[q, i], dx, dy,
             )
         i = 0 if dy < 0 else 1
@@ -254,7 +254,7 @@
         for i in range(2):
             y = 1 if i == 0 else by - 2
             for c in range(3):
-                pa[i, c] = u[q * 3 + c, pl.ds(row_of(0, y), bx, stride=PITCH), :]
+                pa[i, c] = us[q][c, pl.ds(row_of(0, y), bx, stride=PITCH), :]
         for dx, dy in sides_x + sides_y:
             @pl.when(there(dx, dy))
             def _(dx=dx, dy=dy):
@@ -275,7 +275,7 @@
                     i = 0 if dy < 0 else 1
                     y = by + 1 if i == 0 else -2
                     for c in range(3):
-                        u[q * 3 + c, pl.ds(row_of(0, y), bx, stride=PITCH), :] = ra[q, i, c]
+                        us[q][c, pl.ds(row_of(0, y), bx, stride=PITCH), :] = ra[q, i, c]
 
     def tough_copy(r):
         return pltpu.make_async_remote_copy(
@@ -283,7 +283,7 @@
             device_id={"section": lax.rem(me_s + ns - r, ns)}, device_id_type=MESH,
         )
 
-    send_b(lf, 0, 1, None)
+    send_b(lf, 1, None)
     for r in range(1, ns):
         tough_copy(r).start()
 
@@ -301,36 +301,36 @@
         return pl.ds(start, by) if stride == 1 else pl.ds(start, bx, stride=stride)
 
     case = index_ref[0]
-    vector = [loads_ref[case, c] for c in range(3)]
-
-    take_b(lf, 0, 1, None)
+    vector = [loads_ref[c, case] for c in range(3)]
+
+    take_b(lf, 1, None)
 
     def fill(x, carry):
         here = pl.ds(x * PITCH, PITCH)
         load = lf[0, here, :]
         for c in range(3):
-            u[c, here, :] = load * vector[c]
+            u0[c, here, :] = load * vector[c]
         return carry
 
     lax.fori_loop(0, bx + 2 * HALO, fill, 0, unroll=2)
     tail = pl.ds((bx + 2 * HALO) * PITCH, 8)
     for c in range(3):
-        u[c, tail, :] = lf[0, tail, :] * vector[c]
+        u0[c, tail, :] = lf[0, tail, :] * vector[c]
 
     def first_flow(x, carry):
         start = row_of(x, 0)
         trace = (
-            u[0, pl.ds(start + PITCH, by), :] - u[0, pl.ds(start - PITCH, by), :]
-            + u[1, pl.ds(start + 1, by), :] - u[1, pl.ds(start - 1, by), :]
-        )
-        value = u[2, pl.ds(start, by), :]
+            u0[0, pl.ds(start + PITCH, by), :] - u0[0, pl.ds(start - PITCH, by), :]
+            + u0[1, pl.ds(start + 1, by), :] - u0[1, pl.ds(start - 1, by), :]
+        )
+        value = u0[2, pl.ds(start, by), :]
         trace = trace + (from_high(value, 0.0) - from_low(value, 0.0))
-        df[1, pl.ds(start, by), :] = kk[pl.ds(start, by), :] * (0.5 * trace)
+        df0[1, pl.ds(start, by), :] = kk[pl.ds(start, by), :] * (0.5 * trace)
         return carry
 
     lax.fori_loop(0, bx, first_flow, 0, unroll=4)
-    sent_b(lf, 0, 1)
-    send_b(df, 0, 0, 0)
+    sent_b(lf, 1)
+    send_b(df0, 0, u0)
     copies[3].wait()
 
     def move(p, start, stride, out_x=None):
@@ -347,18 +347,18 @@
         w_xm, w_xp, w_ym, w_yp = k + k_xm, k + k_xp, k + k_ym, k + k_yp
         w_zm = jnp.where(at_low, 0.0, k + k_zm)
         w_zp = jnp.where(at_high, 0.0, k + k_zp)
-        flow = 2 * p + 1
-        middle_flow = at(df, 0, flow)
+        df, u = dfs[p], us[p]
+        middle_flow = at(df, 0, 1)
         slopes = (
-            at(df, PITCH, flow) - at(df, -PITCH, flow),
-            at(df, 1, flow) - at(df, -1, flow),
+            at(df, PITCH, 1) - at(df, -PITCH, 1),
+            at(df, 1, 1) - at(df, -1, 1),
             from_high(middle_flow, 0.0) - from_low(middle_flow, 0.0),
         )
         fixed = at(lf, 0, 1) > 0.5
         load = at(lf, 0, 0)
         squares = None
         for c in range(3):
-            f = p * 3 + c
+            f = c
             here = at(u, 0, f)
             total_c = (
                 w_xm * at(u, -PITCH, f) + w_xp * at(u, PITCH, f)
@@ -368,7 +368,7 @@
             residual = total_c - total * here + 2.0 * slopes[c]
             relaxed = here + relax_weight * residual / (total + pairs[c])
             new = jnp.where(fixed, load * vector[c], relaxed)
-            u[q * 3 + c, span(start, stride), :] = new
+            us[q][c, span(start, stride), :] = new
             if out_x is not None and out_x[0]:
                 disp_ref[0, c, out_x[1]] = new
             square = residual * residual
@@ -379,11 +379,11 @@
         q = 1 - p
         start = row_of(x, 0)
         def at(offset, f):
-            return u[f, pl.ds(start + offset, by), :]
+            return us[q][f, pl.ds(start + offset, by), :]
 
         grads = []
         for c in range(3):
-            f = q * 3 + c
+            f = c
             here = at(0, f)
             grads.append((
                 at(PITCH, f) - at(-PITCH, f),
@@ -397,7 +397,7 @@
             0.5 * (grads[1][2] + grads[2][1]),
         )
         def near(offset):
-            return df[2 * p, pl.ds(start + offset, by), :]
+            return dfs[p][0, pl.ds(start + offset, by), :]
 
         here = near(0)
         beside = (
@@ -412,26 +412,26 @@
             dam_ref[0, x] = renewed
         else:
             stiff = (1.0 - renewed) * (1.0 - renewed) + stiff_floor
-            df[2 * q, pl.ds(start, by), :] = renewed
+            dfs[q][0, pl.ds(start, by), :] = renewed
             kk[pl.ds(start, by), :] = stiff
-            df[2 * q + 1, pl.ds(start, by), :] = stiff * (0.5 * trace)
+            dfs[q][1, pl.ds(start, by), :] = stiff * (0.5 * trace)
 
     columns = lax.broadcasted_iota(jnp.int32, (1, nz), 1)
 
-    def sweep(r, table, last):
-        p = lax.rem(r, 2)
+    def sweep(r, p, table, first=False, last=False):
         q = 1 - p
-        take_b(df, 2 * p, p, p)
-
-        def move_own(x, total):
-            return total + move(p, row_of(x, 0), 1, (last, x))
+        take_b(dfs[p], p, us[p])
+
+        def move_own(i, total):
+            for x in range(group):
+                total = total + move(p, row_of(i * group + x, 0), 1, (last, i * group + x))
+            return total
 
         squares = lax.fori_loop(
-            0, bx, move_own, jnp.zeros((by, nz), jnp.float32), unroll=4
+            0, bx // group, move_own, jnp.zeros((by, nz), jnp.float32)
         )
         if not last:
-            @pl.when(r > 0)
-            def _():
+            if not first:
                 sent_a(p)
             send_a(q)
         else:
@@ -446,21 +446,17 @@
         for y in (-1, by):
             move(p, row_of(0, y), PITCH)
 
-        if last:
+        if not first:
             tough_copy(r).wait_recv()
-        else:
-            @pl.when(r > 0)
-            def _():
-                tough_copy(r).wait_recv()
 
         def heal_own(x, carry):
             heal(p, r, x, last)
             return carry
 
-        lax.fori_loop(0, bx, heal_own, 0, unroll=4)
-        sent_b(df, 2 * p, p)
+        lax.fori_loop(0, bx, heal_own, 0, unroll=group)
+        sent_b(dfs[p], p)
         if not last:
-            send_b(df, 2 * q, q, q)
+            send_b(dfs[q], q, us[q])
             take_a(q)
         return table
 
@@ -490,10 +486,12 @@
 
         lax.fori_loop(1, nx * ny, start, 0)
 
-    table = lax.fori_loop(
-        0, ns - 1, lambda r, t: sweep(r, t, False), jnp.zeros((1, nz), jnp.float32)
-    )
-    sweep(jnp.int32(ns - 1), table, True)
+    def two_sweeps(i, table):
+        return sweep(2 * i + 2, 0, sweep(2 * i + 1, 1, table))
+
+    table = sweep(0, 0, jnp.zeros((1, nz), jnp.float32), first=True)
+    table = lax.fori_loop(0, (ns - 2) // 2, two_sweeps, table)
+    sweep(ns - 1, 1, table, last=True)
 
     for r in range(1, ns):
         tough_copy(r).wait_send()
@@ -519,8 +517,10 @@
     flat = (bx * by, nz)
     f32 = jnp.float32
     scratch = [
-        pltpu.VMEM((6, rows, nz), f32),
-        pltpu.VMEM((4, rows, nz), f32),
+        pltpu.VMEM((3, rows, nz), f32),
+        pltpu.VMEM((3, rows, nz), f32),
+        pltpu.VMEM((2, rows, nz), f32),
+        pltpu.VMEM((2, rows, nz), f32),
         pltpu.VMEM((rows, nz), f32),
         pltpu.VMEM((2, rows, nz), f32),
         pltpu.VMEM(flat, jnp.int32),
@@ -562,7 +562,7 @@
         name="sweeps",
     )(
         load_index,
-        load_table,
+        load_table.T,
         toughness.reshape(flat),
         clamp_mask.reshape(flat),
         load_mask.reshape(flat),

time: 98.1 us -> 68.3 us (0.70)
  the two profiles are of different devices: /device:TPU:16 before, /device:TPU:24 now
where the time goes in v2:
time: 68.3 us; the launch traced here: 68.2 us
  Pallas kernels  63.9 us (94%)
  local copies, waits for them, and re-layouts  2.98 us (4%)
  between operations  1.3 us (2%)
    pallas_call x1, Pallas kernels, on_device(): pl.pallas_call(functools.partial(kernel, sizes, bx, by, cells), out_shape...  63.9 us
    unnamed x7, local copies, waits for them, and re-layouts  2.98 us

profile of v2, /device:TPU:24, one launch (start us, length us, event | category | flops | bytes accessed | tf_op | source)
XLA Modules:
  0.0 68.2 jit_solution(6218912390004666726)
XLA Ops:
  1.3 63.9 %sweeps.1 = (f32[1,3,16,16,128]{4,3,2,1,0:T(8,128)}, f32[1,16,16,128]{3,2,1,0:T(8,128)}, f32[1,8]{1,0:T(1,128)}) custom-call(s32[1]{0:T(128)S(6)} %copy.12.index_ref, f32[3,64]{1,0:T(4,128)} %bitcast.9, f32[256,128]{1,0:T(8,128)} %bitcast.5, s32[256,128]{1,0:T(8,128)} %bitcast.6, s32[256,128]{1,0:T(8,128)} %bitcast.7, s32[256,128]{1,0:T(8,128)} %bitcast.8), custom_call_target="tpu_custom_call" | custom-call | tf_op jit(solution)/shard_map/sweeps/pallas_call | solution.py:551
  65.2 0.0 copy-start
  65.2 1.8 %copy.13 = f32[1,3,16,16,128]{4,3,2,1,0:T(8,128)} copy(f32[1,3,16,16,128]{4,3,2,1,0:T(8,128)} %get-tuple-element.6) | data formatting | bytes 786432
  67.0 0.0 copy-done
  67.0 0.0 copy-start.1
  67.0 0.7 copy.14
  67.7 0.0 copy-done.1
  67.7 0.5 copy.15
Async XLA Ops:
  65.2 1.8 %copy-start = (f32[1,16,16,128]{3,2,1,0:T(8,128)S(1)}, f32[1,16,16,128]{3,2,1,0:T(8,128)}, u32[]{:S(2)}) copy-start(f32[1,16,16,128]{3,2,1,0:T(8,128)} %get-tuple-element.7) | copy-start | bytes 393220
  67.0 0.7 copy-start.1

commit v3 on v2

--- a/solution.py
+++ b/solution.py
@@ -27,7 +27,6 @@
 PITCH = 24
 LEAD = 8
 HALO = 2
-group = 8
 
 
 def row_of(x, y):
@@ -71,7 +70,7 @@
     sizes, bx, by, cells,
     index_ref, loads_ref, tough_ref, clamp_ref, load_ref, crack_ref,
     disp_ref, dam_ref, table_ref,
-    u0, u1, df0, df1, kk, lf, clamp_v, load_v, crack_v, g,
+    u0, u1, df0, df1, kk0, kk1, lf, clamp_v, load_v, crack_v, g,
     pa, ra, pb, rb, pc, rc, row_v, rows_v,
     local_sem, a_send, a_recv, b_send, b_recv, t_send, t_recv, s_send, s_recv,
 ):
@@ -80,7 +79,7 @@
     me_x = lax.axis_index("gx")
     me_y = lax.axis_index("gy")
     nz = u0.shape[-1]
-    us, dfs = (u0, u1), (df0, df1)
+    us, dfs, kks = (u0, u1), (df0, df1), (kk0, kk1)
 
     copies = [
         pltpu.make_async_copy(source, target, local_sem.at[i])
@@ -99,7 +98,8 @@
                 ref[i, pl.ds(start, size), :] = jnp.zeros((size, nz), jnp.float32)
         lf[0, pl.ds(start, size), :] = jnp.zeros((size, nz), jnp.float32)
         lf[1, pl.ds(start, size), :] = jnp.ones((size, nz), jnp.float32)
-        kk[pl.ds(start, size), :] = jnp.full((size, nz), outside_stiff, jnp.float32)
+        for ref in kks:
+            ref[pl.ds(start, size), :] = jnp.full((size, nz), outside_stiff, jnp.float32)
 
     def there(dx, dy):
         return (
@@ -135,7 +135,7 @@
         lf[0, here, :] = load
         lf[1, here, :] = jnp.maximum(load, clamp)
         df0[0, here, :] = crack
-        kk[here, :] = (1.0 - crack) * (1.0 - crack) + stiff_floor
+        kk0[here, :] = (1.0 - crack) * (1.0 - crack) + stiff_floor
         return carry
 
     lax.fori_loop(0, bx, begin, 0, unroll=4)
@@ -219,7 +219,7 @@
                             value = rb[q, i, f * HALO + layer]
                             field[f, strip, :] = value
                             if current is not None and f == 0:
-                                kk[strip, :] = (1.0 - value) * (1.0 - value) + stiff_floor
+                                kks[q][strip, :] = (1.0 - value) * (1.0 - value) + stiff_floor
                 elif dy != 0:
                     i = corners.index((dx, dy))
                     row = row_of(bx if dx < 0 else -1, by if dy < 0 else -1)
@@ -227,14 +227,14 @@
                         for c in range(3):
                             current[c, pl.ds(row, 1), :] = rc[q, i, pl.ds(c, 1), :]
                         value = rc[q, i, pl.ds(3, 1), :]
-                        kk[pl.ds(row, 1), :] = (1.0 - value) * (1.0 - value) + stiff_floor
+                        kks[q][pl.ds(row, 1), :] = (1.0 - value) * (1.0 - value) + stiff_floor
                     for f in range(2):
                         field[f, pl.ds(row, 1), :] = rc[q, i, pl.ds(3 + f, 1), :]
         if current is not None:
             for x in (-2, -1, bx, bx + 1):
                 here = pl.ds(row_of(x, 0), by)
                 value = field[0, here, :]
-                kk[here, :] = (1.0 - value) * (1.0 - value) + stiff_floor
+                kks[q][here, :] = (1.0 - value) * (1.0 - value) + stiff_floor
 
     def a_copy(q, dx, dy):
         if dy == 0:
@@ -325,7 +325,7 @@
         )
         value = u0[2, pl.ds(start, by), :]
         trace = trace + (from_high(value, 0.0) - from_low(value, 0.0))
-        df0[1, pl.ds(start, by), :] = kk[pl.ds(start, by), :] * (0.5 * trace)
+        df0[1, pl.ds(start, by), :] = kk0[pl.ds(start, by), :] * (0.5 * trace)
         return carry
 
     lax.fori_loop(0, bx, first_flow, 0, unroll=4)
@@ -333,8 +333,9 @@
     send_b(df0, 0, u0)
     copies[3].wait()
 
-    def move(p, start, stride, out_x=None):
-        q = 1 - p
+    def move(p, start, stride):
+        df, u, kk = dfs[p], us[p], kks[p]
+
         def at(ref, offset, *lead):
             return ref[(*lead, span(start + offset, stride), slice(None))]
 
@@ -347,7 +348,6 @@
         w_xm, w_xp, w_ym, w_yp = k + k_xm, k + k_xp, k + k_ym, k + k_yp
         w_zm = jnp.where(at_low, 0.0, k + k_zm)
         w_zp = jnp.where(at_high, 0.0, k + k_zp)
-        df, u = dfs[p], us[p]
         middle_flow = at(df, 0, 1)
         slopes = (
             at(df, PITCH, 1) - at(df, -PITCH, 1),
@@ -358,36 +358,32 @@
         load = at(lf, 0, 0)
         squares = None
         for c in range(3):
-            f = c
-            here = at(u, 0, f)
+            here = at(u, 0, c)
             total_c = (
-                w_xm * at(u, -PITCH, f) + w_xp * at(u, PITCH, f)
-                + w_ym * at(u, -1, f) + w_yp * at(u, 1, f)
+                w_xm * at(u, -PITCH, c) + w_xp * at(u, PITCH, c)
+                + w_ym * at(u, -1, c) + w_yp * at(u, 1, c)
                 + w_zm * pltpu.roll(here, 1, 1) + w_zp * pltpu.roll(here, nz - 1, 1)
             )
             residual = total_c - total * here + 2.0 * slopes[c]
             relaxed = here + relax_weight * residual / (total + pairs[c])
-            new = jnp.where(fixed, load * vector[c], relaxed)
-            us[q][c, span(start, stride), :] = new
-            if out_x is not None and out_x[0]:
-                disp_ref[0, c, out_x[1]] = new
+            us[1 - p][c, span(start, stride), :] = jnp.where(fixed, load * vector[c], relaxed)
             square = residual * residual
             squares = square if squares is None else squares + square
         return jnp.where(fixed, 0.0, squares)
 
-    def heal(p, r, x, last):
+    def heal(p, r, start, stride, held):
         q = 1 - p
-        start = row_of(x, 0)
-        def at(offset, f):
-            return us[q][f, pl.ds(start + offset, by), :]
+        df, u = dfs[p], us[q]
+
+        def at(ref, offset, *lead):
+            return ref[(*lead, span(start + offset, stride), slice(None))]
 
         grads = []
         for c in range(3):
-            f = c
-            here = at(0, f)
+            here = at(u, 0, c)
             grads.append((
-                at(PITCH, f) - at(-PITCH, f),
-                at(1, f) - at(-1, f),
+                at(u, PITCH, c) - at(u, -PITCH, c),
+                at(u, 1, c) - at(u, -1, c),
                 from_high(here, 0.0) - from_low(here, 0.0),
             ))
         energy, trace = twice_energy(
@@ -396,68 +392,91 @@
             0.5 * (grads[0][2] + grads[2][0]),
             0.5 * (grads[1][2] + grads[2][1]),
         )
-        def near(offset):
-            return dfs[p][0, pl.ds(start + offset, by), :]
-
-        here = near(0)
+        here = at(df, 0, 0)
         beside = (
-            near(PITCH) + near(-PITCH) + near(1) + near(-1)
+            at(df, PITCH, 0) + at(df, -PITCH, 0) + at(df, 1, 0) + at(df, -1, 0)
             + from_high(here, 0.0) + from_low(here, 0.0)
         )
-        held = pl.ds(x * by, by)
         rate = g[r, held, :]
         renewed = (energy + rate * beside) / (energy + 7.0 * rate)
         renewed = jnp.where(crack_v[held, :] > 0, 1.0, renewed)
-        if last:
-            dam_ref[0, x] = renewed
-        else:
-            stiff = (1.0 - renewed) * (1.0 - renewed) + stiff_floor
-            dfs[q][0, pl.ds(start, by), :] = renewed
-            kk[pl.ds(start, by), :] = stiff
-            dfs[q][1, pl.ds(start, by), :] = stiff * (0.5 * trace)
+        stiff = (1.0 - renewed) * (1.0 - renewed) + stiff_floor
+        to = span(start, stride)
+        dfs[q][0, to, :] = renewed
+        dfs[q][1, to, :] = stiff * (0.5 * trace)
+        kks[q][to, :] = stiff
 
     columns = lax.broadcasted_iota(jnp.int32, (1, nz), 1)
+    y_of = lax.broadcasted_iota(jnp.int32, (by, nz), 0)
+    at_rim = (y_of == 0) | (y_of == by - 1)
+
+    def in_groups(low, high, body, total):
+        steps = 2 if (high - low) % 2 == 0 else 1
+        size = (high - low) // steps
+
+        def step(i, total):
+            for j in range(size):
+                added = body(low + i * size + j)
+                total = total if added is None else total + added
+            return total
+
+        return lax.fori_loop(0, steps, step, total)
 
     def sweep(r, p, table, first=False, last=False):
         q = 1 - p
+
+        def move_slab(x):
+            return move(p, row_of(x, 0), 1)
+
+        def move_strip(y):
+            return move(p, row_of(0, y), PITCH)
+
+        def heal_slab(x):
+            heal(p, r, row_of(x, 0), 1, pl.ds(x * by, by))
+
+        def heal_strip(y):
+            heal(p, r, row_of(0, y), PITCH, pl.ds(y, bx, stride=by))
+
+        nothing = jnp.zeros((by, nz), jnp.float32)
+        squares = in_groups(1, bx - 1, move_slab, nothing)
+        if not first:
+            tough_copy(r).wait_recv()
+        in_groups(2, bx - 2, heal_slab, 0)
+
+        if not first:
+            take_a(p)
         take_b(dfs[p], p, us[p])
-
-        def move_own(i, total):
-            for x in range(group):
-                total = total + move(p, row_of(i * group + x, 0), 1, (last, i * group + x))
-            return total
-
-        squares = lax.fori_loop(
-            0, bx // group, move_own, jnp.zeros((by, nz), jnp.float32)
-        )
+        for x in (0, bx - 1):
+            squares = squares + move_slab(x)
+        squares = jnp.where(at_rim, 0.0, squares)
+        for y in (0, by - 1):
+            squares = squares + move_strip(y)
+        for x in (-1, bx):
+            move_slab(x)
+        for y in (-1, by):
+            move_strip(y)
+        if not first:
+            sent_a(p)
         if not last:
-            if not first:
-                sent_a(p)
             send_a(q)
-        else:
-            sent_a(p)
         total = jnp.sum(jnp.sum(squares, axis=0, keepdims=True), axis=1, keepdims=True)
         column = lax.rem(me_s + r, ns)
         table = jnp.where(columns == column, jnp.broadcast_to(total, (1, nz)), table)
         if last:
             spread_sums(table)
-        for x in (-1, bx):
-            move(p, row_of(x, 0), 1)
-        for y in (-1, by):
-            move(p, row_of(0, y), PITCH)
-
-        if not first:
-            tough_copy(r).wait_recv()
-
-        def heal_own(x, carry):
-            heal(p, r, x, last)
-            return carry
-
-        lax.fori_loop(0, bx, heal_own, 0, unroll=group)
+        for x in (0, 1, bx - 2, bx - 1):
+            heal_slab(x)
+        for y in (0, 1, by - 2, by - 1):
+            heal_strip(y)
         sent_b(dfs[p], p)
         if not last:
             send_b(dfs[q], q, us[q])
-            take_a(q)
+        else:
+            for x in range(bx):
+                here = pl.ds(row_of(x, 0), by)
+                for c in range(3):
+                    disp_ref[0, c, x] = us[q][c, here, :]
+                dam_ref[0, x] = dfs[q][0, here, :]
         return table
 
     def sums_copy(t):
@@ -521,6 +540,7 @@
         pltpu.VMEM((3, rows, nz), f32),
         pltpu.VMEM((2, rows, nz), f32),
         pltpu.VMEM((2, rows, nz), f32),
+        pltpu.VMEM((rows, nz), f32),
         pltpu.VMEM((rows, nz), f32),
         pltpu.VMEM((2, rows, nz), f32),
         pltpu.VMEM(flat, jnp.int32),
@@ -551,9 +571,9 @@
     return pl.pallas_call(
         functools.partial(kernel, sizes, bx, by, cells),
         out_shape=(
-            jax.ShapeDtypeStruct((1, 3, bx, by, nz), f32),
-            jax.ShapeDtypeStruct((1, bx, by, nz), f32),
-            jax.ShapeDtypeStruct((1, ns), f32),
+            pltpu.VMEM((1, 3, bx, by, nz), f32),
+            pltpu.VMEM((1, bx, by, nz), f32),
+            pltpu.VMEM((1, ns), f32),
         ),
         in_specs=[smem, smem, hbm, hbm, hbm, hbm],
         out_specs=(vmem, vmem, vmem),

time: 68.3 us -> 60 us (0.88)
  the two profiles are of different devices: /device:TPU:24 before, /device:TPU:8 now
where the time goes in v3:
time: 60 us; the launch traced here: 59.9 us
  Pallas kernels  56.7 us (94%)
  local copies, waits for them, and re-layouts  1.91 us (3%)
  between operations  1.29 us (2%)
    pallas_call x1, Pallas kernels, on_device(): pl.pallas_call(functools.partial(kernel, sizes, bx, by, cells), out_shape...  56.7 us
    unnamed x3, local copies, waits for them, and re-layouts  1.91 us

profile of v3, /device:TPU:8, one launch (start us, length us, event | category | flops | bytes accessed | tf_op | source)
XLA Modules:
  0.0 59.9 jit_solution(4820988391101238802)
XLA Ops:
  1.3 56.7 %sweeps.1 = (f32[1,3,16,16,128]{4,3,2,1,0:T(8,128)S(1)}, f32[1,16,16,128]{3,2,1,0:T(8,128)S(1)}, f32[1,8]{1,0:T(1,128)S(1)}) custom-call(s32[1]{0:T(128)S(6)} %copy.15.index_ref, f32[3,64]{1,0:T(4,128)} %bitcast.9, f32[256,128]{1,0:T(8,128)} %bitcast.5, s32[256,128]{1,0:T(8,128)} %bitcast.6, s32[256,128]{1,0:T(8,128)} %bitcast.7, s32[256,128]{1,0:T(8,128)} %bitcast.8), custom_call_target="tpu_custom_call" | custom-call | tf_op jit(solution)/shard_map/sweeps/pallas_call | solution.py:571
  58.0 0.7 %copy.12 = f32[1,3,16,16,128]{4,3,2,1,0:T(8,128)} copy(f32[1,3,16,16,128]{4,3,2,1,0:T(8,128)S(1)} %get-tuple-element.3) | data formatting | bytes 786432
  58.7 0.5 copy.14
  59.2 0.7 %copy.13 = f32[1,16,16,128]{3,2,1,0:T(8,128)} copy(f32[1,16,16,128]{3,2,1,0:T(8,128)S(1)} %get-tuple-element.4) | data formatting | bytes 262144

commit v4 on v3

--- a/solution.py
+++ b/solution.py
@@ -27,10 +27,11 @@
 PITCH = 24
 LEAD = 8
 HALO = 2
+BORDER = 3
 
 
 def row_of(x, y):
-    return (x + HALO) * PITCH + LEAD + y
+    return (x + BORDER) * PITCH + LEAD + y
 
 
 def polynomial(coefficients, t):
@@ -71,27 +72,37 @@
     index_ref, loads_ref, tough_ref, clamp_ref, load_ref, crack_ref,
     disp_ref, dam_ref, table_ref,
     u0, u1, df0, df1, kk0, kk1, lf, clamp_v, load_v, crack_v, g,
-    pa, ra, pb, rb, pc, rc, row_v, rows_v,
-    local_sem, a_send, a_recv, b_send, b_recv, t_send, t_recv, s_send, s_recv,
+    pa, ra, pb, rb, pc, rc, pm, pcm, hx, hm, hcm, row_v, rows_v, wv, stage_u, stage_d,
+    local_sem, m_send, m_recv, w_sem, o_send, o_recv, a_send, a_recv, b_send, b_recv, t_send, t_recv, s_send, s_recv,
 ):
     ns, nx, ny = sizes
     me_s = lax.axis_index("section")
     me_x = lax.axis_index("gx")
     me_y = lax.axis_index("gy")
+    swapped = lax.rem(me_x, 2)
+
+    def place(case, x):
+        return case + lax.rem(x + 2, 2) * (1 - 2 * lax.rem(case, 2))
+
+    me_v = place(me_s, me_x)
+
+    def neighbour_id(dx, dy):
+        return {"section": place(me_v, me_x + dx), "gx": me_x + dx, "gy": me_y + dy}
+
     nz = u0.shape[-1]
     us, dfs, kks = (u0, u1), (df0, df1), (kk0, kk1)
 
     copies = [
         pltpu.make_async_copy(source, target, local_sem.at[i])
         for i, (source, target) in enumerate(
-            ((load_ref, load_v), (clamp_ref, clamp_v), (crack_ref, crack_v), (tough_ref, g.at[0]))
+            ((load_ref, load_v), (clamp_ref, clamp_v), (crack_ref, crack_v))
         )
     ]
     for copy in copies:
         copy.start()
 
-    halo_pieces = [(i * PITCH, 8) for i in range(bx + 2 * HALO + 1)]
-    halo_pieces += [(row_of(x, 0), by) for x in (-2, -1, bx, bx + 1)]
+    halo_pieces = [(i * PITCH, 8) for i in range(bx + 2 * BORDER + 1)]
+    halo_pieces += [(row_of(x, 0), by) for x in (-3, -2, -1, bx, bx + 1, bx + 2)]
     for start, size in halo_pieces:
         for ref in us + dfs:
             for i in range(ref.shape[0]):
@@ -116,13 +127,16 @@
         @pl.when(there(dx, dy))
         def _(dx=dx, dy=dy):
             pl.semaphore_signal(
-                barrier, inc=1, device_id={"gx": me_x + dx, "gy": me_y + dy}, device_id_type=MESH
+                barrier, inc=1, device_id=neighbour_id(dx, dy), device_id_type=MESH
             )
     for r in range(1, ns):
         pl.semaphore_signal(
             barrier, inc=1, device_id={"section": lax.rem(me_s + r, ns)}, device_id_type=MESH
         )
 
+    case = index_ref[0]
+    for c in range(3):
+        wv[0, c] = jnp.full((8, nz), loads_ref[c, case], jnp.float32)
     for i in (0, 1, 2):
         copies[i].wait()
 
@@ -140,6 +154,19 @@
 
     lax.fori_loop(0, bx, begin, 0, unroll=4)
 
+    for i in range(2):
+        for ref, n, first in ((load_v, 3, 0), (crack_v, 2, 3), (clamp_v, 1, 5)):
+            for layer in range(n):
+                y = layer if i == 0 else by - n + layer
+                pm[i, first + layer] = ref[pl.ds(y, bx, stride=by), :]
+    for i, (dx, dy) in enumerate(corners):
+        x, deep_x = (0, 1) if dx < 0 else (bx - 1, bx - 2)
+        y, deep_y = (0, 1) if dy < 0 else (by - 1, by - 2)
+        for j, (ref, at_x, at_y) in enumerate((
+            (load_v, x, y), (load_v, deep_x, y), (load_v, x, deep_y), (crack_v, x, y),
+        )):
+            pcm[i, pl.ds(j, 1), :] = ref[pl.ds(at_x * by + at_y, 1), :]
+
     across = 1 + (me_x > 0).astype(jnp.int32) + (me_x < nx - 1).astype(jnp.int32)
     along = 1 + (me_y > 0).astype(jnp.int32) + (me_y < ny - 1).astype(jnp.int32)
     pl.semaphore_wait(barrier, across * along - 1 + (ns - 1))
@@ -147,7 +174,7 @@
     def remote(source, target, send, recv, dx, dy):
         return pltpu.make_async_remote_copy(
             src_ref=source, dst_ref=target, send_sem=send, recv_sem=recv,
-            device_id={"gx": me_x + dx, "gy": me_y + dy}, device_id_type=MESH,
+            device_id=neighbour_id(dx, dy), device_id_type=MESH,
         )
 
     def b_copies(field, q, dx, dy):
@@ -277,15 +304,58 @@
                     for c in range(3):
                         us[q][c, pl.ds(row_of(0, y), bx, stride=PITCH), :] = ra[q, i, c]
 
+    def tough_target(r):
+        return place(lax.rem(me_s + ns - r, ns), me_x)
+
     def tough_copy(r):
         return pltpu.make_async_remote_copy(
             src_ref=tough_ref, dst_ref=g.at[r], send_sem=t_send.at[r], recv_sem=t_recv.at[r],
-            device_id={"section": lax.rem(me_s + ns - r, ns)}, device_id_type=MESH,
-        )
-
-    send_b(lf, 1, None)
-    for r in range(1, ns):
-        tough_copy(r).start()
+            device_id={"section": tough_target(r)}, device_id_type=MESH,
+        )
+
+    def tough_arrived(r):
+        pltpu.make_async_copy(tough_ref, g.at[r], t_recv.at[r]).wait()
+
+    masks = (load_v, crack_v, clamp_v)
+    layers = (3, 2, 1)
+    parts = tuple((ref, n, sum(layers[:i])) for i, (ref, n) in enumerate(zip(masks, layers)))
+
+    def m_copies(dx, dy):
+        if dy == 0:
+            i = 0 if dx < 0 else 1
+            return [
+                remote(
+                    ref.at[pl.ds((0 if dx < 0 else bx - n) * by, n * by), :],
+                    hx.at[i, pl.ds(first * by, n * by), :],
+                    m_send.at[3 * i + j], m_recv.at[3 * i + j], dx, dy,
+                )
+                for j, (ref, n, first) in enumerate(parts)
+            ]
+        if dx == 0:
+            i = 0 if dy < 0 else 1
+            return [remote(pm.at[i], hm.at[i], m_send.at[6 + i], m_recv.at[6 + i], dx, dy)]
+        i = corners.index((dx, dy))
+        return [remote(pcm.at[i], hcm.at[i], m_send.at[8 + i], m_recv.at[8 + i], dx, dy)]
+
+    for dx, dy in order_b:
+        @pl.when(there(dx, dy))
+        def _(dx=dx, dy=dy):
+            for copy in m_copies(dx, dy):
+                copy.start()
+    partner = me_s + 1 - 2 * lax.rem(me_s, 2)
+    w_copy = pltpu.make_async_remote_copy(
+        src_ref=wv.at[0], dst_ref=wv.at[1], send_sem=w_sem.at[0], recv_sem=w_sem.at[1],
+        device_id={"section": partner}, device_id_type=MESH,
+    )
+    w_copy.start()
+    for r in range(ns):
+        @pl.when(tough_target(r) == me_s)
+        def _(r=r):
+            pltpu.make_async_copy(tough_ref, g.at[r], t_recv.at[r]).start()
+
+        @pl.when(tough_target(r) != me_s)
+        def _(r=r):
+            tough_copy(r).start()
 
     lane = lax.broadcasted_iota(jnp.int32, (by, nz), 1)
     at_low = lane == 0
@@ -300,38 +370,103 @@
     def span(start, stride):
         return pl.ds(start, by) if stride == 1 else pl.ds(start, bx, stride=stride)
 
-    case = index_ref[0]
-    vector = [loads_ref[c, case] for c in range(3)]
-
-    take_b(lf, 1, None)
+    def as_float(value):
+        return value.astype(jnp.float32)
+
+    def put_crack(where, crack):
+        crack = as_float(crack)
+        df0[0, where, :] = crack
+        kk0[where, :] = (1.0 - crack) * (1.0 - crack) + stiff_floor
+
+    def outward(low, n, layer, size):
+        return size + layer if low else layer - n
+
+    w_copy.wait_recv()
+    for dx, dy in order_b:
+        @pl.when(there(-dx, -dy))
+        def _(dx=dx, dy=dy):
+            for copy in m_copies(dx, dy):
+                copy.wait_recv()
+            if dy == 0:
+                i, low = (0, True) if dx < 0 else (1, False)
+                for layer in range(3):
+                    here = pl.ds(row_of(outward(low, 3, layer, bx), 0), by)
+                    lf[0, here, :] = as_float(hx[i, pl.ds(layer * by, by), :])
+                for layer in range(2):
+                    here = pl.ds(row_of(outward(low, 2, layer, bx), 0), by)
+                    put_crack(here, hx[i, pl.ds((3 + layer) * by, by), :])
+                near = 0 if low else 2
+                here = pl.ds(row_of(bx if low else -1, 0), by)
+                lf[1, here, :] = as_float(jnp.maximum(
+                    hx[i, pl.ds(near * by, by), :], hx[i, pl.ds(5 * by, by), :]
+                ))
+            elif dx == 0:
+                i, low = (0, True) if dy < 0 else (1, False)
+                for layer in range(3):
+                    y = outward(low, 3, layer, by)
+                    lf[0, pl.ds(row_of(0, y), bx, stride=PITCH), :] = as_float(hm[i, layer])
+                for layer in range(2):
+                    y = outward(low, 2, layer, by)
+                    put_crack(pl.ds(row_of(0, y), bx, stride=PITCH), hm[i, 3 + layer])
+                near = 0 if low else 2
+                y = by if low else -1
+                lf[1, pl.ds(row_of(0, y), bx, stride=PITCH), :] = as_float(
+                    jnp.maximum(hm[i, near], hm[i, 5])
+                )
+            else:
+                i = corners.index((dx, dy))
+                x, far_x = (bx, bx + 1) if dx < 0 else (-1, -2)
+                y, far_y = (by, by + 1) if dy < 0 else (-1, -2)
+                for j, (at_x, at_y) in enumerate(((x, y), (far_x, y), (x, far_y))):
+                    lf[0, pl.ds(row_of(at_x, at_y), 1), :] = as_float(hcm[i, pl.ds(j, 1), :])
+                put_crack(pl.ds(row_of(x, y), 1), hcm[i, pl.ds(3, 1), :])
+
+    vector = [wv[swapped, c] for c in range(3)]
 
     def fill(x, carry):
-        here = pl.ds(x * PITCH, PITCH)
-        load = lf[0, here, :]
-        for c in range(3):
-            u0[c, here, :] = load * vector[c]
+        for here in (x * PITCH, x * PITCH + 8, x * PITCH + 16):
+            load = lf[0, pl.ds(here, 8), :]
+            for c in range(3):
+                u0[c, pl.ds(here, 8), :] = load * vector[c]
         return carry
 
-    lax.fori_loop(0, bx + 2 * HALO, fill, 0, unroll=2)
-    tail = pl.ds((bx + 2 * HALO) * PITCH, 8)
+    lax.fori_loop(0, bx + 2 * BORDER, fill, 0, unroll=2)
+    tail = pl.ds((bx + 2 * BORDER) * PITCH, 8)
     for c in range(3):
         u0[c, tail, :] = lf[0, tail, :] * vector[c]
-
-    def first_flow(x, carry):
-        start = row_of(x, 0)
-        trace = (
-            u0[0, pl.ds(start + PITCH, by), :] - u0[0, pl.ds(start - PITCH, by), :]
-            + u0[1, pl.ds(start + 1, by), :] - u0[1, pl.ds(start - 1, by), :]
-        )
-        value = u0[2, pl.ds(start, by), :]
-        trace = trace + (from_high(value, 0.0) - from_low(value, 0.0))
-        df0[1, pl.ds(start, by), :] = kk0[pl.ds(start, by), :] * (0.5 * trace)
+    vector = [jnp.concatenate([v, v], axis=0) for v in vector]
+
+    def first_flow(start, stride, count):
+        def at(offset, c):
+            if stride == 1:
+                return u0[c, pl.ds(start + offset, count), :]
+            return u0[c, pl.ds(start + offset, count, stride=stride), :]
+
+        to = pl.ds(start, count) if stride == 1 else pl.ds(start, count, stride=stride)
+        value = at(0, 2)
+        high = jnp.where(at_high[:count], 0.0, pltpu.roll(value, nz - 1, 1))
+        low = jnp.where(at_low[:count], 0.0, pltpu.roll(value, 1, 1))
+        trace = at(PITCH, 0) - at(-PITCH, 0) + at(1, 1) - at(-1, 1) + (high - low)
+        df0[1, to, :] = kk0[to, :] * (0.5 * trace)
+
+    def first_flow_own(x, carry):
+        first_flow(row_of(x, 0), 1, by)
         return carry
 
-    lax.fori_loop(0, bx, first_flow, 0, unroll=4)
-    sent_b(lf, 1)
-    send_b(df0, 0, u0)
-    copies[3].wait()
+    lax.fori_loop(0, bx, first_flow_own, 0, unroll=4)
+    for dx, dy in order_b:
+        @pl.when(there(-dx, -dy))
+        def _(dx=dx, dy=dy):
+            xs = (bx, bx + 1) if dx < 0 else (-2, -1)
+            ys = (by, by + 1) if dy < 0 else (-2, -1)
+            if dy == 0:
+                for x in xs:
+                    first_flow(row_of(x, 0), 1, by)
+            elif dx == 0:
+                for y in ys:
+                    first_flow(row_of(0, y), PITCH, bx)
+            else:
+                first_flow(row_of(bx if dx < 0 else -1, by if dy < 0 else -1), 1, 1)
 
     def move(p, start, stride):
         df, u, kk = dfs[p], us[p], kks[p]
@@ -439,13 +574,12 @@
 
         nothing = jnp.zeros((by, nz), jnp.float32)
         squares = in_groups(1, bx - 1, move_slab, nothing)
-        if not first:
-            tough_copy(r).wait_recv()
+        tough_arrived(r)
         in_groups(2, bx - 2, heal_slab, 0)
 
         if not first:
             take_a(p)
-        take_b(dfs[p], p, us[p])
+            take_b(dfs[p], p, us[p])
         for x in (0, bx - 1):
             squares = squares + move_slab(x)
         squares = jnp.where(at_rim, 0.0, squares)
@@ -460,44 +594,82 @@
         if not last:
             send_a(q)
         total = jnp.sum(jnp.sum(squares, axis=0, keepdims=True), axis=1, keepdims=True)
-        column = lax.rem(me_s + r, ns)
+        column = lax.rem(me_v + r, ns)
         table = jnp.where(columns == column, jnp.broadcast_to(total, (1, nz)), table)
         if last:
             spread_sums(table)
+            give_displacement(us[q])
         for x in (0, 1, bx - 2, bx - 1):
             heal_slab(x)
         for y in (0, 1, by - 2, by - 1):
             heal_strip(y)
-        sent_b(dfs[p], p)
+        if not first:
+            sent_b(dfs[p], p)
         if not last:
             send_b(dfs[q], q, us[q])
         else:
+            give_damage(dfs[q])
+        return table
+
+    def give(stage, out_ref, i):
+        return pltpu.make_async_remote_copy(
+            src_ref=stage, dst_ref=out_ref.at[0], send_sem=o_send.at[i], recv_sem=o_recv.at[i],
+            device_id={"section": partner}, device_id_type=MESH,
+        )
+
+    give_u = give(stage_u, disp_ref, 0)
+    give_d = give(stage_d, dam_ref, 1)
+
+    def give_displacement(u):
+        @pl.when(swapped == 0)
+        def _():
             for x in range(bx):
-                here = pl.ds(row_of(x, 0), by)
                 for c in range(3):
-                    disp_ref[0, c, x] = us[q][c, here, :]
-                dam_ref[0, x] = dfs[q][0, here, :]
-        return table
+                    disp_ref[0, c, x] = u[c, pl.ds(row_of(x, 0), by), :]
+
+        @pl.when(swapped == 1)
+        def _():
+            for x in range(bx):
+                for c in range(3):
+                    stage_u[c, x] = u[c, pl.ds(row_of(x, 0), by), :]
+            give_u.start()
+
+    def give_damage(df):
+        @pl.when(swapped == 0)
+        def _():
+            for x in range(bx):
+                dam_ref[0, x] = df[0, pl.ds(row_of(x, 0), by), :]
+
+        @pl.when(swapped == 1)
+        def _():
+            for x in range(bx):
+                stage_d[x] = df[0, pl.ds(row_of(x, 0), by), :]
+            give_d.start()
+
+    me = me_x * ny + me_y
 
     def sums_copy(t):
-        me = me_x * ny + me_y
         to = lax.rem(me + t, nx * ny)
         return pltpu.make_async_remote_copy(
             src_ref=row_v, dst_ref=rows_v.at[me], send_sem=s_send.at[t], recv_sem=s_recv.at[t],
-            device_id={"gx": to // ny, "gy": lax.rem(to, ny)}, device_id_type=MESH,
-        )
-
-    def from_copy(t):
-        me = me_x * ny + me_y
+            device_id={"section": me_v, "gx": to // ny, "gy": lax.rem(to, ny)},
+            device_id_type=MESH,
+        )
+
+    def sums_arrived(t):
         source = lax.rem(me + nx * ny - t, nx * ny)
-        return pltpu.make_async_remote_copy(
-            src_ref=row_v, dst_ref=rows_v.at[source], send_sem=s_send.at[t], recv_sem=s_recv.at[t],
-            device_id={"gx": me_x, "gy": me_y}, device_id_type=MESH,
-        )
+        pltpu.make_async_copy(row_v, rows_v.at[source], s_recv.at[t]).wait()
 
     def spread_sums(table):
         row_v[...] = table
-        rows_v[me_x * ny + me_y] = table
+
+        @pl.when(swapped == 0)
+        def _():
+            rows_v[me] = table
+
+        @pl.when(swapped == 1)
+        def _():
+            sums_copy(0).start()
 
         def start(t, carry):
             sums_copy(t).start()
@@ -512,12 +684,29 @@
     table = lax.fori_loop(0, (ns - 2) // 2, two_sweeps, table)
     sweep(ns - 1, 1, table, last=True)
 
-    for r in range(1, ns):
-        tough_copy(r).wait_send()
+    w_copy.wait_send()
+    for dx, dy in order_b:
+        @pl.when(there(dx, dy))
+        def _(dx=dx, dy=dy):
+            for copy in m_copies(dx, dy):
+                copy.wait_send()
+
+    for r in range(ns):
+        @pl.when(tough_target(r) != me_s)
+        def _(r=r):
+            tough_copy(r).wait_send()
+
+    @pl.when(swapped == 1)
+    def _():
+        sums_copy(0).wait_send()
+        sums_arrived(0)
+        for copy in (give_u, give_d):
+            copy.wait_send()
+            copy.wait_recv()
 
     def finish(t, carry):
         sums_copy(t).wait_send()
-        from_copy(t).wait_recv()
+        sums_arrived(t)
         return carry
 
     lax.fori_loop(1, nx * ny, finish, 0)
@@ -532,7 +721,7 @@
     ns, nx, ny = sizes
     bx, by, nz = clamp_mask.shape
     cells = float(clamp_mask.size * nx * ny)
-    rows = (bx + 2 * HALO) * PITCH + LEAD
+    rows = (bx + 2 * BORDER) * PITCH + LEAD
     flat = (bx * by, nz)
     f32 = jnp.float32
     scratch = [
@@ -553,9 +742,22 @@
         pltpu.VMEM((2, 2, 2 * HALO, bx, nz), f32),
         pltpu.VMEM((4, 8, nz), f32),
         pltpu.VMEM((2, 4, 8, nz), f32),
+        pltpu.VMEM((2, 6, bx, nz), jnp.int32),
+        pltpu.VMEM((4, 8, nz), jnp.int32),
+        pltpu.VMEM((2, 6 * by, nz), jnp.int32),
+        pltpu.VMEM((2, 6, bx, nz), jnp.int32),
+        pltpu.VMEM((4, 8, nz), jnp.int32),
         pltpu.VMEM((1, nz), f32),
         pltpu.VMEM((nx * ny, 1, nz), f32),
-        pltpu.SemaphoreType.DMA((4,)),
+        pltpu.VMEM((2, 3, 8, nz), f32),
+        pltpu.VMEM((3, bx, by, nz), f32),
+        pltpu.VMEM((bx, by, nz), f32),
+        pltpu.SemaphoreType.DMA((3,)),
+        pltpu.SemaphoreType.DMA((12,)),
+        pltpu.SemaphoreType.DMA((12,)),
+        pltpu.SemaphoreType.DMA((2,)),
+        pltpu.SemaphoreType.DMA((2,)),
+        pltpu.SemaphoreType.DMA((2,)),
         pltpu.SemaphoreType.DMA((2, 4)),
         pltpu.SemaphoreType.DMA((2, 4)),
         pltpu.SemaphoreType.DMA((2, 10)),

time: 60 us -> 57.7 us (0.962)
  the two profiles are of different devices: /device:TPU:8 before, /device:TPU:1 now
where the time goes in v4:
time: 57.7 us; the launch traced here: 57.6 us
  Pallas kernels  54.4 us (94%)
  local copies, waits for them, and re-layouts  1.91 us (3%)
  between operations  1.29 us (2%)
    pallas_call x1, Pallas kernels, on_device(): pl.pallas_call(functools.partial(kernel, sizes, bx, by, cells), out_shape...  54.4 us
    unnamed x3, local copies, waits for them, and re-layouts  1.91 us

profile of v4, /device:TPU:1, one launch (start us, length us, event | category | flops | bytes accessed | tf_op | source)
XLA Modules:
  0.0 57.6 jit_solution(3714953641454740090)
XLA Ops:
  1.3 54.4 %sweeps.1 = (f32[1,3,16,16,128]{4,3,2,1,0:T(8,128)S(1)}, f32[1,16,16,128]{3,2,1,0:T(8,128)S(1)}, f32[1,8]{1,0:T(1,128)S(1)}) custom-call(s32[1]{0:T(128)S(6)} %copy.15.index_ref, f32[3,64]{1,0:T(4,128)} %bitcast.9, f32[256,128]{1,0:T(8,128)} %bitcast.5, s32[256,128]{1,0:T(8,128)} %bitcast.6, s32[256,128]{1,0:T(8,128)} %bitcast.7, s32[256,128]{1,0:T(8,128)} %bitcast.8), custom_call_target="tpu_custom_call" | custom-call | tf_op jit(solution)/shard_map/sweeps/pallas_call | solution.py:773
  55.7 0.7 %copy.12 = f32[1,3,16,16,128]{4,3,2,1,0:T(8,128)} copy(f32[1,3,16,16,128]{4,3,2,1,0:T(8,128)S(1)} %get-tuple-element.3) | data formatting | bytes 786432
  56.4 0.5 copy.14
  57.0 0.7 %copy.13 = f32[1,16,16,128]{3,2,1,0:T(8,128)} copy(f32[1,16,16,128]{3,2,1,0:T(8,128)S(1)} %get-tuple-element.4) | data formatting | bytes 262144

commit v5 on v4

--- a/solution.py
+++ b/solution.py
@@ -231,8 +231,8 @@
                 for copy in b_copies(field, q, dx, dy):
                     copy.wait_send()
 
-    def take_b(field, q, current):
-        for dx, dy in order_b:
+    def take_b(field, q, current, directions):
+        for dx, dy in directions:
             @pl.when(there(-dx, -dy))
             def _(dx=dx, dy=dy):
                 for copy in b_copies(field, q, dx, dy):
@@ -257,7 +257,7 @@
                         kks[q][pl.ds(row, 1), :] = (1.0 - value) * (1.0 - value) + stiff_floor
                     for f in range(2):
                         field[f, pl.ds(row, 1), :] = rc[q, i, pl.ds(3 + f, 1), :]
-        if current is not None:
+        if directions is not corners:
             for x in (-2, -1, bx, bx + 1):
                 here = pl.ds(row_of(x, 0), by)
                 value = field[0, here, :]
@@ -578,21 +578,23 @@
         in_groups(2, bx - 2, heal_slab, 0)
 
         if not first:
-            take_a(p)
-            take_b(dfs[p], p, us[p])
+            take_b(dfs[p], p, us[p], sides_x + sides_y)
         for x in (0, bx - 1):
             squares = squares + move_slab(x)
         squares = jnp.where(at_rim, 0.0, squares)
         for y in (0, by - 1):
             squares = squares + move_strip(y)
+        if not first:
+            sent_a(p)
+        if not last:
+            send_a(q)
+        if not first:
+            take_a(p)
+            take_b(dfs[p], p, us[p], corners)
         for x in (-1, bx):
             move_slab(x)
         for y in (-1, by):
             move_strip(y)
-        if not first:
-            sent_a(p)
-        if not last:
-            send_a(q)
         total = jnp.sum(jnp.sum(squares, axis=0, keepdims=True), axis=1, keepdims=True)
         column = lax.rem(me_v + r, ns)
         table = jnp.where(columns == column, jnp.broadcast_to(total, (1, nz)), table)
@@ -648,20 +650,34 @@
 
     me = me_x * ny + me_y
 
+    def hops(offset):
+        return sum(min(o, n - o) for o, n in zip(offset, (nx, ny)))
+
+    offsets = sorted(
+        ((tx, ty) for tx in range(nx) for ty in range(ny)), key=lambda o: (-hops(o), o)
+    )
+
     def sums_copy(t):
-        to = lax.rem(me + t, nx * ny)
+        tx, ty = offsets[t]
         return pltpu.make_async_remote_copy(
             src_ref=row_v, dst_ref=rows_v.at[me], send_sem=s_send.at[t], recv_sem=s_recv.at[t],
-            device_id={"section": me_v, "gx": to // ny, "gy": lax.rem(to, ny)},
+            device_id={
+                "section": me_v, "gx": lax.rem(me_x + tx, nx), "gy": lax.rem(me_y + ty, ny),
+            },
             device_id_type=MESH,
         )
 
     def sums_arrived(t):
-        source = lax.rem(me + nx * ny - t, nx * ny)
+        tx, ty = offsets[t]
+        source = lax.rem(me_x + nx - tx, nx) * ny + lax.rem(me_y + ny - ty, ny)
         pltpu.make_async_copy(row_v, rows_v.at[source], s_recv.at[t]).wait()
+
+    here_t = nx * ny - 1
 
     def spread_sums(table):
         row_v[...] = table
+        for t in range(here_t):
+            sums_copy(t).start()
 
         @pl.when(swapped == 0)
         def _():
@@ -669,13 +685,7 @@
 
         @pl.when(swapped == 1)
         def _():
-            sums_copy(0).start()
-
-        def start(t, carry):
-            sums_copy(t).start()
-            return carry
-
-        lax.fori_loop(1, nx * ny, start, 0)
+            sums_copy(here_t).start()
 
     def two_sweeps(i, table):
         return sweep(2 * i + 2, 0, sweep(2 * i + 1, 1, table))
@@ -698,23 +708,32 @@
 
     @pl.when(swapped == 1)
     def _():
-        sums_copy(0).wait_send()
-        sums_arrived(0)
+        sums_copy(here_t).wait_send()
+        sums_arrived(here_t)
         for copy in (give_u, give_d):
             copy.wait_send()
             copy.wait_recv()
 
-    def finish(t, carry):
+    for t in range(here_t):
         sums_copy(t).wait_send()
         sums_arrived(t)
-        return carry
-
-    lax.fori_loop(1, nx * ny, finish, 0)
     everything = rows_v[0]
     for i in range(1, nx * ny):
         everything = everything + rows_v[i]
     result = jnp.sqrt(everything * (0.25 / (3.0 * cells)))
     table_ref[...] = result[:, :ns]
+
+
+def write_out(*refs):
+    sources, targets, sem = refs[:3], refs[3:6], refs[6]
+    copies = [
+        pltpu.make_async_copy(source, target, sem.at[i])
+        for i, (source, target) in enumerate(zip(sources, targets))
+    ]
+    for copy in copies:
+        copy.start()
+    for copy in copies:
+        copy.wait()
 
 
 def on_device(sizes, load_index, load_table, toughness, clamp_mask, load_mask, crack_mask):
@@ -770,7 +789,7 @@
     smem = pl.BlockSpec(memory_space=pltpu.SMEM)
     vmem = pl.BlockSpec(memory_space=pltpu.VMEM)
     hbm = pl.BlockSpec(memory_space=pl.ANY)
-    return pl.pallas_call(
+    results = pl.pallas_call(
         functools.partial(kernel, sizes, bx, by, cells),
         out_shape=(
             pltpu.VMEM((1, 3, bx, by, nz), f32),
@@ -790,6 +809,15 @@
         load_mask.reshape(flat),
         crack_mask.reshape(flat),
     )
+    results = [pltpu.with_memory_space_constraint(value, pltpu.VMEM) for value in results]
+    return pl.pallas_call(
+        write_out,
+        out_shape=tuple(pltpu.HBM(value.shape, f32) for value in results),
+        in_specs=[vmem] * 3,
+        out_specs=(hbm,) * 3,
+        scratch_shapes=[pltpu.SemaphoreType.DMA((3,))],
+        name="write_out",
+    )(*results)
 
 
 def solution(mesh):

time: 57.7 us -> 55.3 us (0.958)
  local copies, waits for them, and re-layouts: 1.91 us -> 0 us
    unnamed x3 -> x0, local copies, waits for them, and re-layouts: 1.91 us -> none
    pallas_call x1, Pallas kernels: 54.4 us -> 53.1 us  [on_device(): pl.pallas_call(functools.partial(kernel, sizes, bx, by, cells), out_shape...]
    pallas_call x0 -> x1, Pallas kernels: none -> 0.82 us  [on_device(): pl.pallas_call(write_out, out_shape=tuple((pltpu.HBM(value.shape, f32) fo...]
where the time goes in v5:
time: 55.3 us; the launch traced here: 55.2 us
  Pallas kernels  53.9 us (97%)
  between operations  1.28 us (2%)
    pallas_call x1, Pallas kernels, on_device(): pl.pallas_call(functools.partial(kernel, sizes, bx, by, cells), out_shape...  53.1 us

profile of v5, /device:TPU:1, one launch (start us, length us, event | category | flops | bytes accessed | tf_op | source)
XLA Modules:
  0.0 55.2 jit_solution(1191459369633161394)
XLA Ops:
  1.3 53.1 %sweeps.1 = (f32[1,3,16,16,128]{4,3,2,1,0:T(8,128)S(1)}, f32[1,16,16,128]{3,2,1,0:T(8,128)S(1)}, f32[1,8]{1,0:T(1,128)S(1)}) custom-call(s32[1]{0:T(128)S(6)} %copy.9.index_ref, f32[3,64]{1,0:T(4,128)} %bitcast.9, f32[256,128]{1,0:T(8,128)} %bitcast.5, s32[256,128]{1,0:T(8,128)} %bitcast.6, s32[256,128]{1,0:T(8,128)} %bitcast.7, s32[256,128]{1,0:T(8,128)} %bitcast.8), custom_call_target="tpu_custom_call" | custom-call | tf_op jit(solution)/shard_map/sweeps/pallas_call | solution.py:792
  54.4 0.8 %write_out.1 = (f32[1,3,16,16,128]{4,3,2,1,0:T(8,128)}, f32[1,16,16,128]{3,2,1,0:T(8,128)}, f32[1,8]{1,0:T(1,128)}) custom-call(f32[1,3,16,16,128]{4,3,2,1,0:T(8,128)S(1)} %get-tuple-element.6.refs_0_, f32[1,16,16,128]{3,2,1,0:T(8,128)S(1)} %get-tuple-element.7.refs_1_, f32[1,8]{1,0:T(1,128)S(1)} %get-tuple-element.8.refs_2_), custom_call_target="tpu_custom_call" | custom-call | tf_op jit(solution)/shard_map/write_out/pallas_call | solution.py:813

commit v6 on v5

--- a/solution.py
+++ b/solution.py
@@ -69,10 +69,10 @@
 
 def kernel(
     sizes, bx, by, cells,
-    index_ref, loads_ref, tough_ref, clamp_ref, load_ref, crack_ref,
+    index_ref, loads_hbm, tough_ref, clamp_ref, load_ref, crack_ref,
     disp_ref, dam_ref, table_ref,
     u0, u1, df0, df1, kk0, kk1, lf, clamp_v, load_v, crack_v, g,
-    pa, ra, pb, rb, pc, rc, pm, pcm, hx, hm, hcm, row_v, rows_v, wv, stage_u, stage_d,
+    pa, ra, pb, rb, pc, rc, pm, pcm, hx, hm, hcm, row_v, rows_v, wv, stage_u, stage_d, loads_ref,
     local_sem, m_send, m_recv, w_sem, o_send, o_recv, a_send, a_recv, b_send, b_recv, t_send, t_recv, s_send, s_recv,
 ):
     ns, nx, ny = sizes
@@ -95,7 +95,10 @@
     copies = [
         pltpu.make_async_copy(source, target, local_sem.at[i])
         for i, (source, target) in enumerate(
-            ((load_ref, load_v), (clamp_ref, clamp_v), (crack_ref, crack_v))
+            (
+                (load_ref, load_v), (clamp_ref, clamp_v), (crack_ref, crack_v),
+                (loads_hbm, loads_ref),
+            )
         )
     ]
     for copy in copies:
@@ -134,6 +137,7 @@
             barrier, inc=1, device_id={"section": lax.rem(me_s + r, ns)}, device_id_type=MESH
         )
 
+    copies[3].wait()
     case = index_ref[0]
     for c in range(3):
         wv[0, c] = jnp.full((8, nz), loads_ref[c, case], jnp.float32)
@@ -584,6 +588,14 @@
         squares = jnp.where(at_rim, 0.0, squares)
         for y in (0, by - 1):
             squares = squares + move_strip(y)
+
+        def with_sums(table):
+            total = jnp.sum(jnp.sum(squares, axis=0, keepdims=True), axis=1, keepdims=True)
+            column = lax.rem(me_v + r, ns)
+            return jnp.where(columns == column, jnp.broadcast_to(total, (1, nz)), table)
+
+        if last:
+            spread_sums(with_sums(table))
         if not first:
             sent_a(p)
         if not last:
@@ -595,11 +607,7 @@
             move_slab(x)
         for y in (-1, by):
             move_strip(y)
-        total = jnp.sum(jnp.sum(squares, axis=0, keepdims=True), axis=1, keepdims=True)
-        column = lax.rem(me_v + r, ns)
-        table = jnp.where(columns == column, jnp.broadcast_to(total, (1, nz)), table)
         if last:
-            spread_sums(table)
             give_displacement(us[q])
         for x in (0, 1, bx - 2, bx - 1):
             heal_slab(x)
@@ -609,6 +617,7 @@
             sent_b(dfs[p], p)
         if not last:
             send_b(dfs[q], q, us[q])
+            table = with_sums(table)
         else:
             give_damage(dfs[q])
         return table
@@ -771,7 +780,8 @@
         pltpu.VMEM((2, 3, 8, nz), f32),
         pltpu.VMEM((3, bx, by, nz), f32),
         pltpu.VMEM((bx, by, nz), f32),
-        pltpu.SemaphoreType.DMA((3,)),
+        pltpu.SMEM(load_table.shape[::-1], f32),
+        pltpu.SemaphoreType.DMA((4,)),
         pltpu.SemaphoreType.DMA((12,)),
         pltpu.SemaphoreType.DMA((12,)),
         pltpu.SemaphoreType.DMA((2,)),
@@ -786,7 +796,6 @@
         pltpu.SemaphoreType.DMA((nx * ny,)),
         pltpu.SemaphoreType.DMA((nx * ny,)),
     ]
-    smem = pl.BlockSpec(memory_space=pltpu.SMEM)
     vmem = pl.BlockSpec(memory_space=pltpu.VMEM)
     hbm = pl.BlockSpec(memory_space=pl.ANY)
     results = pl.pallas_call(
@@ -796,7 +805,7 @@
             pltpu.VMEM((1, bx, by, nz), f32),
             pltpu.VMEM((1, ns), f32),
         ),
-        in_specs=[smem, smem, hbm, hbm, hbm, hbm],
+        in_specs=[pl.BlockSpec(memory_space=pltpu.SMEM)] + [hbm] * 5,
         out_specs=(vmem, vmem, vmem),
         scratch_shapes=scratch,
         compiler_params=pltpu.CompilerParams(collective_id=0, has_side_effects=True),

time: 55.3 us -> 54.3 us (0.982)
  Pallas kernels: 53.9 us -> 52.9 us
    pallas_call x1, Pallas kernels: 53.1 us -> 52.1 us  [on_device(): pl.pallas_call(functools.partial(kernel, sizes, bx, by, cells), out_shape...]
where the time goes in v6:
time: 54.3 us; the launch traced here: 54.2 us
  Pallas kernels  52.9 us (97%)
  between operations  1.28 us (2%)
    pallas_call x1, Pallas kernels, on_device(): pl.pallas_call(functools.partial(kernel, sizes, bx, by, cells), out_shape...  52.1 us

profile of v6, /device:TPU:1, one launch (start us, length us, event | category | flops | bytes accessed | tf_op | source)
XLA Modules:
  0.0 54.2 jit_solution(6601202066062462602)
XLA Ops:
  1.3 52.1 %sweeps.1 = (f32[1,3,16,16,128]{4,3,2,1,0:T(8,128)S(1)}, f32[1,16,16,128]{3,2,1,0:T(8,128)S(1)}, f32[1,8]{1,0:T(1,128)S(1)}) custom-call(s32[1]{0:T(128)S(6)} %copy.9.index_ref, f32[3,64]{1,0:T(4,128)} %bitcast.9, f32[256,128]{1,0:T(8,128)} %bitcast.5, s32[256,128]{1,0:T(8,128)} %bitcast.6, s32[256,128]{1,0:T(8,128)} %bitcast.7, s32[256,128]{1,0:T(8,128)} %bitcast.8), custom_call_target="tpu_custom_call" | custom-call | tf_op jit(solution)/shard_map/sweeps/pallas_call | solution.py:801
  53.4 0.8 %write_out.1 = (f32[1,3,16,16,128]{4,3,2,1,0:T(8,128)}, f32[1,16,16,128]{3,2,1,0:T(8,128)}, f32[1,8]{1,0:T(1,128)}) custom-call(f32[1,3,16,16,128]{4,3,2,1,0:T(8,128)S(1)} %get-tuple-element.6.refs_0_, f32[1,16,16,128]{3,2,1,0:T(8,128)S(1)} %get-tuple-element.7.refs_1_, f32[1,8]{1,0:T(1,128)S(1)} %get-tuple-element.8.refs_2_), custom_call_target="tpu_custom_call" | custom-call | tf_op jit(solution)/shard_map/write_out/pallas_call | solution.py:822

commit v7 on v6

--- a/solution.py
+++ b/solution.py
@@ -107,7 +107,7 @@
     halo_pieces = [(i * PITCH, 8) for i in range(bx + 2 * BORDER + 1)]
     halo_pieces += [(row_of(x, 0), by) for x in (-3, -2, -1, bx, bx + 1, bx + 2)]
     for start, size in halo_pieces:
-        for ref in us + dfs:
+        for ref in (u1,) + dfs:
             for i in range(ref.shape[0]):
                 ref[i, pl.ds(start, size), :] = jnp.zeros((size, nz), jnp.float32)
         lf[0, pl.ds(start, size), :] = jnp.zeros((size, nz), jnp.float32)
@@ -386,6 +386,39 @@
         return size + layer if low else layer - n
 
     w_copy.wait_recv()
+    narrow = [wv[swapped, c] for c in range(3)]
+
+    def fill(x, carry):
+        for here in (x * PITCH, x * PITCH + 8, x * PITCH + 16):
+            load = lf[0, pl.ds(here, 8), :]
+            for c in range(3):
+                u0[c, pl.ds(here, 8), :] = load * narrow[c]
+        return carry
+
+    lax.fori_loop(0, bx + 2 * BORDER, fill, 0, unroll=2)
+    tail = pl.ds((bx + 2 * BORDER) * PITCH, 8)
+    for c in range(3):
+        u0[c, tail, :] = lf[0, tail, :] * narrow[c]
+    vector = [jnp.concatenate([v, v], axis=0) for v in narrow]
+
+    def first_flow(start, stride, count):
+        def at(offset, c):
+            if stride == 1:
+                return u0[c, pl.ds(start + offset, count), :]
+            return u0[c, pl.ds(start + offset, count, stride=stride), :]
+
+        to = pl.ds(start, count) if stride == 1 else pl.ds(start, count, stride=stride)
+        value = at(0, 2)
+        high = jnp.where(at_high[:count], 0.0, pltpu.roll(value, nz - 1, 1))
+        low = jnp.where(at_low[:count], 0.0, pltpu.roll(value, 1, 1))
+        trace = at(PITCH, 0) - at(-PITCH, 0) + at(1, 1) - at(-1, 1) + (high - low)
+        df0[1, to, :] = kk0[to, :] * (0.5 * trace)
+
+    def first_flow_own(x, carry):
+        first_flow(row_of(x, 0), 1, by)
+        return carry
+
+    lax.fori_loop(1, bx - 1, first_flow_own, 0, unroll=2)
     for dx, dy in order_b:
         @pl.when(there(-dx, -dy))
         def _(dx=dx, dy=dy):
@@ -425,39 +458,16 @@
                     lf[0, pl.ds(row_of(at_x, at_y), 1), :] = as_float(hcm[i, pl.ds(j, 1), :])
                 put_crack(pl.ds(row_of(x, y), 1), hcm[i, pl.ds(3, 1), :])
 
-    vector = [wv[swapped, c] for c in range(3)]
-
-    def fill(x, carry):
-        for here in (x * PITCH, x * PITCH + 8, x * PITCH + 16):
-            load = lf[0, pl.ds(here, 8), :]
-            for c in range(3):
-                u0[c, pl.ds(here, 8), :] = load * vector[c]
-        return carry
-
-    lax.fori_loop(0, bx + 2 * BORDER, fill, 0, unroll=2)
-    tail = pl.ds((bx + 2 * BORDER) * PITCH, 8)
-    for c in range(3):
-        u0[c, tail, :] = lf[0, tail, :] * vector[c]
-    vector = [jnp.concatenate([v, v], axis=0) for v in vector]
-
-    def first_flow(start, stride, count):
-        def at(offset, c):
-            if stride == 1:
-                return u0[c, pl.ds(start + offset, count), :]
-            return u0[c, pl.ds(start + offset, count, stride=stride), :]
-
-        to = pl.ds(start, count) if stride == 1 else pl.ds(start, count, stride=stride)
-        value = at(0, 2)
-        high = jnp.where(at_high[:count], 0.0, pltpu.roll(value, nz - 1, 1))
-        low = jnp.where(at_low[:count], 0.0, pltpu.roll(value, 1, 1))
-        trace = at(PITCH, 0) - at(-PITCH, 0) + at(1, 1) - at(-1, 1) + (high - low)
-        df0[1, to, :] = kk0[to, :] * (0.5 * trace)
-
-    def first_flow_own(x, carry):
+    for x in (0, 1, 2, bx + 3, bx + 4, bx + 5):
+        fill(x, 0)
+    for x in range(bx + 2 * BORDER + 1):
+        lead = pl.ds(x * PITCH, 8)
+        for c in range(3):
+            u0[c, lead, :] = lf[0, lead, :] * narrow[c]
+    for x in (0, bx - 1):
         first_flow(row_of(x, 0), 1, by)
-        return carry
-
-    lax.fori_loop(0, bx, first_flow_own, 0, unroll=4)
+    for y in (0, by - 1):
+        first_flow(row_of(0, y), PITCH, bx)
     for dx, dy in order_b:
         @pl.when(there(-dx, -dy))
         def _(dx=dx, dy=dy):

time: 54.3 us -> 53.9 us (level)
  no operation moved by 1% of the time
where the time goes in v7:
time: 53.9 us; the launch traced here: 53.8 us
  Pallas kernels  52.5 us (97%)
  between operations  1.28 us (2%)
    pallas_call x1, Pallas kernels, on_device(): pl.pallas_call(functools.partial(kernel, sizes, bx, by, cells), out_shape...  51.7 us

profile of v7, /device:TPU:1, one launch (start us, length us, event | category | flops | bytes accessed | tf_op | source)
XLA Modules:
  0.0 53.8 jit_solution(15378327491883310581)
XLA Ops:
  1.3 51.7 %sweeps.1 = (f32[1,3,16,16,128]{4,3,2,1,0:T(8,128)S(1)}, f32[1,16,16,128]{3,2,1,0:T(8,128)S(1)}, f32[1,8]{1,0:T(1,128)S(1)}) custom-call(s32[1]{0:T(128)S(6)} %copy.9.index_ref, f32[3,64]{1,0:T(4,128)} %bitcast.9, f32[256,128]{1,0:T(8,128)} %bitcast.5, s32[256,128]{1,0:T(8,128)} %bitcast.6, s32[256,128]{1,0:T(8,128)} %bitcast.7, s32[256,128]{1,0:T(8,128)} %bitcast.8), custom_call_target="tpu_custom_call" | custom-call | tf_op jit(solution)/shard_map/sweeps/pallas_call | solution.py:811
  53.0 0.8 %write_out.1 = (f32[1,3,16,16,128]{4,3,2,1,0:T(8,128)}, f32[1,16,16,128]{3,2,1,0:T(8,128)}, f32[1,8]{1,0:T(1,128)}) custom-call(f32[1,3,16,16,128]{4,3,2,1,0:T(8,128)S(1)} %get-tuple-element.6.refs_0_, f32[1,16,16,128]{3,2,1,0:T(8,128)S(1)} %get-tuple-element.7.refs_1_, f32[1,8]{1,0:T(1,128)S(1)} %get-tuple-element.8.refs_2_), custom_call_target="tpu_custom_call" | custom-call | tf_op jit(solution)/shard_map/write_out/pallas_call | solution.py:832
